TPU v7x, 512 devices: a whole 4x8x8 slice. The times are simulated.
512 devices in a mesh: fy: 16 (over y, core), fx: 16 (over z, x_hi), blk: 2 (over x_lo).
Axes of the slice: x: 4 (x_hi: 2, x_lo: 2; x = x_hi * 2 + x_lo), y: 8, z: 8, core: 2. Of those that a mesh axis runs over, the one named last changes fastest.
Arguments:
- sky_image: bfloat16 [8, 2048, 2048], P('blk', 'fy', 'fx'), may hold values from -33 to 33
- vis_data: bfloat16 [16, 16, 8, 2, 512], P('fy', 'fx', 'blk'), may hold values from -6 to 6
- interp_weights: bfloat16 [16, 16, 8, 4, 2, 128, 128], P('fy', 'fx'), may hold values from -0.125 to 0.125
- tile_rows: int32 [16, 16, 8, 4, 2], P('fy', 'fx'), may hold values from 0 to 127
- facet_list: int32 [16, 16, 8], P('fy', 'fx'), may hold values from 0 to 15, as said below
- vis_count: int32 [16, 16], P('fy', 'fx'), may hold values from 128 to 512
- wavelet_threshold: float32 [4, 8], P(None, 'blk'), may hold values from 0.05 to 0.5
- spectral_weight: float32 [], replicated, may hold values from 0.1 to 1
Outputs:
- restored: float32 [8, 2048, 2048], P('blk', 'fy', 'fx')
Inputs may be any that keep to these rules, and one draw needn't show every extreme that they name: `facet_list`: the 8 facet numbers of one block are distinct.
All inputs are finite; a program needn't handle non-finite values.
Results may differ from a plain program's by a relative error of at most 0.0035.
Values may be sent and summed in bfloat16 or wider, within the bound.
A program may use at most 64 MiB of HBM per device.

v0:
```python
import math

import jax
import jax.numpy as jnp
from jax import lax
from jax.sharding import PartitionSpec as P

top_precision = lax.Precision.HIGHEST
descent_step = 2.0


def from_everyone(shard, axis):
    copies = jnp.broadcast_to(shard, (lax.axis_size(axis), *shard.shape))
    return lax.all_to_all(copies, axis, split_axis=0, concat_axis=0, tiled=True)


def joined_along(blocks, dim):
    blocks = jnp.moveaxis(blocks, 0, dim)
    shape = blocks.shape
    return blocks.reshape(*shape[:dim], shape[dim] * shape[dim + 1], *shape[dim + 2 :])


def collect(shard, axis, dim):
    blocks = from_everyone(shard, axis)
    return joined_along(blocks, dim)


def side_by_side(arrays, axis, dim, along):
    widths = [math.prod(a.shape[along:]) for a in arrays]
    both = jnp.concatenate(
        [a.reshape(*a.shape[:along], w) for a, w in zip(arrays, widths)], axis=along
    )
    filled = lax.all_gather(both, axis, axis=dim, tiled=True)
    blocks = jnp.split(filled, [sum(widths[:k]) for k in range(1, len(widths))], axis=along)
    return tuple(
        (b.reshape(*filled.shape[:along], *a.shape[along:]) for a, b in zip(arrays, blocks))
    )


def extended(cells, sides, width):
    for axis, dim in sides:
        count = lax.axis_size(axis)
        ends = count - 1
        head = lax.slice_in_dim(cells, 0, width, axis=dim)
        tail = lax.slice_in_dim(cells, cells.shape[dim] - width, cells.shape[dim], axis=dim)
        cells = jnp.concatenate(
            [
                lax.ppermute(tail, axis, [(i, (i + 1) % count) for i in range(ends)]),
                cells,
                lax.ppermute(head, axis, [((i + 1) % count, i) for i in range(ends)]),
            ],
            axis=dim,
        )
    return cells


def dft_tables(length):
    positions = jnp.arange(length, dtype=jnp.int32)
    phases = positions[:, None] * positions[None, :] % length
    angles = phases.astype(jnp.float32) * (2.0 * math.pi / length)
    scaling = 1.0 / math.sqrt(length)
    cosine = jnp.cos(angles) * scaling
    sinus_table = jnp.sin(angles) * scaling
    left_table = jnp.concatenate([cosine, -sinus_table], axis=0)
    right_table = jnp.stack(
        [
            jnp.concatenate([cosine, -sinus_table], axis=1),
            jnp.concatenate([sinus_table, cosine], axis=1),
        ]
    )
    return (left_table, right_table)


def forward_transform(facets, left_table, right_table):
    halfway = jnp.einsum(
        "wy,fcyx->fcwx", left_table.astype(jnp.bfloat16), facets, preferred_element_type=jnp.float32
    ).astype(jnp.bfloat16)
    facet_count, channel_count, doubled, facet_width = halfway.shape
    halfway = halfway.reshape(facet_count, channel_count, 2, doubled // 2, facet_width)
    spectra = jnp.einsum(
        "fcpux,pxw->fcuw",
        halfway,
        right_table.astype(jnp.bfloat16),
        preferred_element_type=jnp.float32,
    )
    return spectra.astype(jnp.bfloat16)


def adjoint_transform(spectrum_grad, left_table, right_table):
    halfway = jnp.einsum("fcuw,pxw->fcpux", spectrum_grad, right_table, precision=top_precision)
    facet_count, channel_count, parts_two, facet_width, other_width = halfway.shape
    halfway = halfway.reshape(facet_count, channel_count, 2 * facet_width, other_width)
    return jnp.einsum("wy,fcwx->fcyx", left_table, halfway, precision=top_precision)


def pick_rows(spectrum_one, row_ids):
    return jnp.take(spectrum_one, row_ids, axis=1)


def block_rows(chosen, block_vis, block_weights, block_tiles, block_count):
    picked = jax.vmap(pick_rows)(chosen, block_tiles)
    facet_count, channel_count, tile_count, slot_count, doubled = picked.shape
    picked = picked.reshape(facet_count, channel_count, tile_count, slot_count, 2, doubled // 2)
    predicted = jnp.einsum(
        "fanjv,fcanpv->cpaj", block_weights, picked, preferred_element_type=jnp.float32
    )
    predicted = predicted.reshape(channel_count, 2, -1)
    live_mask = jnp.arange(predicted.shape[2], dtype=jnp.int32) < block_count
    residual = jnp.where(live_mask, predicted - block_vis.astype(jnp.float32), 0.0).astype(
        jnp.bfloat16
    )
    residual = residual.reshape(channel_count, 2, tile_count, -1)
    contrib = jnp.einsum(
        "fanjv,cpaj->fancpv", block_weights, residual, preferred_element_type=jnp.float32
    )
    return contrib.reshape(facet_count, tile_count, slot_count, channel_count, doubled)


def smooth_axis(values, stride, axis_id):
    widths = [(0, 0), (0, 0), (0, 0)]
    widths[axis_id] = (stride, stride)
    padded = jnp.pad(values, widths)
    length = values.shape[axis_id]
    below_rows = lax.slice_in_dim(padded, 0, length, axis=axis_id)
    above_rows = lax.slice_in_dim(padded, 2 * stride, 2 * stride + length, axis=axis_id)
    return (below_rows + 2.0 * values + above_rows) * 0.25


def smooth_both(values, stride):
    return smooth_axis(smooth_axis(values, stride, 1), stride, 2)


def shrink_matrix(gram_matrix, offset):
    dimension = gram_matrix.shape[0]
    shifted = gram_matrix + offset * jnp.eye(dimension, dtype=jnp.float32)
    positions = jnp.arange(dimension, dtype=jnp.int32)
    columns = []
    for column_id in range(dimension):
        if column_id > 0:
            earlier = jnp.stack(columns, axis=1)
            correction = jnp.sum(earlier * earlier[column_id][None, :], axis=1)
        else:
            correction = jnp.zeros((dimension,), jnp.float32)
        pivot = jnp.sqrt(shifted[column_id, column_id] - correction[column_id])
        column = (shifted[:, column_id] - correction) / pivot
        columns.append(jnp.where(positions >= column_id, column, 0.0))
    factor = jnp.stack(columns, axis=1)
    forward_rows = []
    for row_id in range(dimension):
        accum = gram_matrix[row_id]
        if row_id > 0:
            accum = accum - jnp.sum(
                factor[row_id, :row_id][:, None] * jnp.stack(forward_rows, axis=0), axis=0
            )
        forward_rows.append(accum / factor[row_id, row_id])
    backward_rows = [None] * dimension
    for row_id in range(dimension - 1, -1, -1):
        accum = forward_rows[row_id]
        if row_id < dimension - 1:
            later = jnp.stack(backward_rows[row_id + 1 :], axis=0)
            accum = accum - jnp.sum(factor[row_id + 1 :, row_id][:, None] * later, axis=0)
        backward_rows[row_id] = accum / factor[row_id, row_id]
    return jnp.stack(backward_rows, axis=0)


def body(
    sky_image,
    vis_data,
    interp_weights,
    tile_rows,
    facet_list,
    vis_count,
    wavelet_threshold,
    spectral_weight,
):
    channel_count, facet_width, other_width = sky_image.shape
    left_table, right_table = dft_tables(facet_width)
    chosen_ids = facet_list[0, 0]
    block_tiles = tile_rows[0, 0]
    row_images = collect(sky_image[None], "fx", 0)
    chosen = forward_transform(jnp.take(row_images, chosen_ids, axis=0), left_table, right_table)
    contrib = block_rows(chosen, vis_data[0, 0], interp_weights[0, 0], block_tiles, vis_count[0, 0])
    facet_count, tile_count, slot_count, chan_here, doubled = contrib.shape
    row_total = lax.axis_size("fx")
    selector = (chosen_ids[:, None] == jnp.arange(row_total, dtype=jnp.int32)[None, :]).astype(
        jnp.float32
    )
    flat_rows = contrib.reshape(facet_count, tile_count * slot_count, chan_here, doubled)
    outgoing = jnp.einsum("fk,frcw->krcw", selector, flat_rows, precision=top_precision)
    row_lists, facet_lists = side_by_side((block_tiles[None], chosen_ids[None]), "fx", 0, 2)
    matched = (facet_lists == lax.axis_index("fx")).astype(jnp.int32)
    source_rows = jnp.sum(matched[:, :, None, None] * row_lists, axis=1).reshape(
        row_total, tile_count * slot_count
    )
    incoming = lax.all_to_all(
        outgoing.astype(jnp.bfloat16), "fx", split_axis=0, concat_axis=0, tiled=True
    ).astype(outgoing.dtype)
    placement = (source_rows[..., None] == jnp.arange(doubled // 2, dtype=jnp.int32)).astype(
        jnp.float32
    )
    own_grad = jnp.einsum("jru,jrcw->cuw", placement, incoming, precision=top_precision)
    gradient = adjoint_transform(own_grad[None], left_table, right_table)[0]
    stepped = sky_image.astype(jnp.float32) - descent_step * gradient
    levels = wavelet_threshold.shape[0]
    coarse = stepped
    clipped_sum = jnp.zeros_like(stepped)
    for level_index in range(levels):
        stride = 2**level_index
        padded = extended(coarse.astype(jnp.bfloat16), (("fy", 1), ("fx", 2)), stride).astype(
            coarse.dtype
        )
        smoother = smooth_both(padded, stride)[
            :, stride : stride + facet_width, stride : stride + other_width
        ]
        bound_now = wavelet_threshold[level_index][:, None, None]
        clipped_sum = clipped_sum + jnp.clip(coarse - smoother, -bound_now, bound_now)
        coarse = smoother
    shrunk = stepped - clipped_sum
    offset = spectral_weight * (facet_width * other_width)
    all_channels = collect(shrunk, "blk", 0)
    gram_matrix = jnp.einsum("cyx,dyx->cd", all_channels, all_channels, precision=top_precision)
    matrix = shrink_matrix(gram_matrix, offset)
    own_cols = lax.dynamic_slice_in_dim(
        matrix, lax.axis_index("blk") * channel_count, channel_count, 1
    )
    result = jnp.einsum("cyx,cd->dyx", all_channels, own_cols, precision=top_precision)
    return result


def solution(mesh):
    in_specs = (
        P("blk", "fy", "fx"),
        P("fy", "fx", "blk", None, None),
        P("fy", "fx", None, None, None, None, None),
        P("fy", "fx", None, None, None),
        P("fy", "fx", None),
        P("fy", "fx"),
        P(None, "blk"),
        P(),
    )
    out_specs = P("blk", "fy", "fx")
    return jax.shard_map(body, mesh=mesh, in_specs=in_specs, out_specs=out_specs, check_vma=False)
```

profile of v0, /device:TPU:88, one launch (start us, length us, event | category | flops | bytes accessed | tf_op | source)
XLA Modules:
  0.0 274.3 jit_solution(11221637153390659785)
XLA Ops:
  0.0 2.9 %broadcast_in_dim.57 = bf16[16,1,4,128,128]{4,3,2,1,0:T(8,128)(2,1)} broadcast(bf16[4,128,128]{2,1,0:T(8,128)(2,1)} %param.8), dimensions={2,3,4} | broadcast | bytes 2228224 | tf_op jit(solution)/shard_map/broadcast_in_dim | solution.py:13
  2.9 12.6 %all-to-all-start = ((bf16[16,1,4,128,128]{4,3,2,1,0:T(8,128)(2,1)}), bf16[16,1,4,128,128]{4,3,2,1,0:T(8,128)(2,1)}, u32[]{:S(2)}, u32[]{:S(2)}) async-start(bf16[16,1,4,128,128]{4,3,2,1,0:T(8,128)(2,1)} %broadcast_in_dim.57), calls=%async_computation | async-start | bytes 4194304 | tf_op jit(solution)/shard_map/all_to_all | solution.py:14
  18.8 46.3 %all-to-all-done = bf16[16,1,4,128,128]{4,3,2,1,0:T(8,128)(2,1)} async-done(((bf16[16,1,4,128,128]{4,3,2,1,0:T(8,128)(2,1)}), bf16[16,1,4,128,128]{4,3,2,1,0:T(8,128)(2,1)}, u32[]{:S(2)}, u32[]{:S(2)}) %all-to-all-start) | async-done | bytes 2097184 | tf_op jit(solution)/shard_map/all_to_all | solution.py:14
  65.1 2.3 gather_fusion
  67.4 2.8 %convert_bitcast_fusion = bf16[8,4,256,128]{2,3,1,0:T(8,128)(2,1)} fusion(bf16[8,4,128,128]{3,2,1,0:T(8,128)(2,1)S(1)} %gather_fusion, pred[8]{0:T(512)(128)(4,1)} %compare_and_fusion.1, f32[128,128]{1,0:T(8,128)S(1)} %get-tuple-element.76, f32[128,128]{1,0:T(8,128)S(1)} %get-tuple-element.75), kind=kOutput, calls=%fused_computation.7 | convolution fusion | flops 270139392 | bytes 3276808 | tf_op jit(solution)/shard_map/wy,fcyx->fcwx/dot_general | solution.py:75
  70.2 3.9 %copy.163 = bf16[8,4,256,128]{3,2,1,0:T(8,128)(2,1)} copy(bf16[8,4,256,128]{2,3,1,0:T(8,128)(2,1)} %convert_bitcast_fusion) | data formatting | bytes 4194304 | tf_op jit(solution)/shard_map/reshape | solution.py:79
  74.1 2.3 bitcast_convert_fusion
  76.4 3.0 %copy.119 = bf16[8,4,128,256]{3,1,2,0:T(4,128)(2,1)} copy(bf16[8,4,128,256]{3,2,1,0:T(8,128)(2,1)S(1)} %bitcast_convert_fusion) | data formatting | bytes 4194304 | tf_op jit(solution)/shard_map/convert_element_type | solution.py:86
  79.4 2.4 gather_fusion.1
  81.9 0.8 fusion
  84.0 0.8 copy.126
  84.9 6.0 %all-to-all-start.1 = ((bf16[16,8,4,256]{3,2,1,0:T(4,128)(2,1)}), bf16[16,8,4,256]{3,2,1,0:T(4,128)(2,1)S(1)}, u32[]{:S(2)}, u32[]{:S(2)}) async-start(bf16[16,8,4,256]{3,2,1,0:T(4,128)(2,1)} %copy.126), calls=%async_computation.1 | async-start | bytes 524288 | tf_op jit(solution)/shard_map/all_to_all | solution.py:195
  91.0 38.8 %all_gather.3 = s32[16,8,9]{2,1,0:T(8,128)S(1)} all-gather(s32[1,8,9]{2,1,0:T(8,128)S(1)} %copy.127), channel_id=1, replica_groups=mesh['fy'=16,'fx'=16,'blk'=2] {'fx'}, dimensions={0}, use_global_device_ids=true | all-gather | bytes 4896 | tf_op jit(solution)/shard_map/all_gather | solution.py:33
  130.8 1.0 convolution_bitcast_fusion
  132.4 1.9 collective-permute-start.1
  134.3 2.4 collective-permute-start
  136.7 2.5 collective-permute-done
  139.4 4.5 %collective-permute-start.3 = (bf16[4,130,1]{2,1,0:T(8,128)(2,1)S(1)}, bf16[4,130,1]{2,1,0:T(8,128)(2,1)S(1)}, u32[]{:S(2)}, u32[]{:S(2)}) collective-permute-start(bf16[4,130,1]{2,1,0:T(8,128)(2,1)S(1)} %get-tuple-element.39), channel_id=1, source_target_pairs={{2,0},{4,2},{6,4},{8,6},{10,8},{12,10},{14,12},{16,14},{18,16},{20... | collective-permute-start | bytes 3128 | tf_op jit(solution)/shard_map/ppermute | solution.py:50
  143.9 2.8 %collective-permute-start.2 = (bf16[4,130,1]{2,1,0:T(8,128)(2,1)S(1)}, bf16[4,130,1]{2,1,0:T(8,128)(2,1)S(1)}, u32[]{:S(2)}, u32[]{:S(2)}) collective-permute-start(bf16[4,130,1]{2,1,0:T(8,128)(2,1)S(1)} %get-tuple-element.38), channel_id=1, source_target_pairs={{0,2},{2,4},{4,6},{6,8},{8,10},{10,12},{12,14},{14,16},{16,18},{18... | collective-permute-start | bytes 3128 | tf_op jit(solution)/shard_map/ppermute | solution.py:48
  146.7 2.2 collective-permute-done.3
  149.0 5.1 %collective-permute-done.2 = bf16[4,130,1]{2,1,0:T(8,128)(2,1)S(1)} collective-permute-done((bf16[4,130,1]{2,1,0:T(8,128)(2,1)S(1)}, bf16[4,130,1]{2,1,0:T(8,128)(2,1)S(1)}, u32[]{:S(2)}, u32[]{:S(2)}) %collective-permute-start.2) | collective-permute-done | bytes 1072 | tf_op jit(solution)/shard_map/ppermute | solution.py:48
  155.2 1.9 collective-permute-start.5
  157.1 2.4 collective-permute-start.4
  159.5 2.5 collective-permute-done.4
  162.2 4.1 %collective-permute-start.7 = (bf16[4,132,2]{2,1,0:T(8,128)(2,1)S(1)}, bf16[4,132,2]{2,1,0:T(8,128)(2,1)S(1)}, u32[]{:S(2)}, u32[]{:S(2)}) collective-permute-start(bf16[4,132,2]{2,1,0:T(8,128)(2,1)S(1)} %get-tuple-element.37), channel_id=1, source_target_pairs={{2,0},{4,2},{6,4},{8,6},{10,8},{12,10},{14,12},{16,14},{18,16},{20... | collective-permute-start | bytes 6344 | tf_op jit(solution)/shard_map/ppermute | solution.py:50
  166.2 3.5 %collective-permute-start.6 = (bf16[4,132,2]{2,1,0:T(8,128)(2,1)S(1)}, bf16[4,132,2]{2,1,0:T(8,128)(2,1)S(1)}, u32[]{:S(2)}, u32[]{:S(2)}) collective-permute-start(bf16[4,132,2]{2,1,0:T(8,128)(2,1)S(1)} %get-tuple-element.36), channel_id=1, source_target_pairs={{0,2},{2,4},{4,6},{6,8},{8,10},{10,12},{12,14},{14,16},{16,18},{18... | collective-permute-start | bytes 6344 | tf_op jit(solution)/shard_map/ppermute | solution.py:48
  169.7 2.4 collective-permute-done.7
  172.1 4.7 %collective-permute-done.6 = bf16[4,132,2]{2,1,0:T(8,128)(2,1)S(1)} collective-permute-done((bf16[4,132,2]{2,1,0:T(8,128)(2,1)S(1)}, bf16[4,132,2]{2,1,0:T(8,128)(2,1)S(1)}, u32[]{:S(2)}, u32[]{:S(2)}) %collective-permute-start.6) | collective-permute-done | bytes 2144 | tf_op jit(solution)/shard_map/ppermute | solution.py:48
  177.8 1.9 collective-permute-start.9
  179.8 2.4 collective-permute-start.8
  182.2 2.5 collective-permute-done.8
  184.8 3.2 %collective-permute-start.11 = (bf16[4,136,4]{2,1,0:T(8,128)(2,1)S(1)}, bf16[4,136,4]{2,1,0:T(8,128)(2,1)S(1)}, u32[]{:S(2)}, u32[]{:S(2)}) collective-permute-start(bf16[4,136,4]{2,1,0:T(8,128)(2,1)S(1)} %get-tuple-element.35), channel_id=1, source_target_pairs={{2,0},{4,2},{6,4},{8,6},{10,8},{12,10},{14,12},{16,14},{18,16},{20... | collective-permute-start | bytes 13064 | tf_op jit(solution)/shard_map/ppermute | solution.py:50
  188.1 4.1 %collective-permute-start.10 = (bf16[4,136,4]{2,1,0:T(8,128)(2,1)S(1)}, bf16[4,136,4]{2,1,0:T(8,128)(2,1)S(1)}, u32[]{:S(2)}, u32[]{:S(2)}) collective-permute-start(bf16[4,136,4]{2,1,0:T(8,128)(2,1)S(1)} %get-tuple-element.34), channel_id=1, source_target_pairs={{0,2},{2,4},{4,6},{6,8},{8,10},{10,12},{12,14},{14,16},{16,18},{18... | collective-permute-start | bytes 13064 | tf_op jit(solution)/shard_map/ppermute | solution.py:48
  192.2 2.6 collective-permute-done.11
  194.8 3.7 %collective-permute-done.10 = bf16[4,136,4]{2,1,0:T(8,128)(2,1)S(1)} collective-permute-done((bf16[4,136,4]{2,1,0:T(8,128)(2,1)S(1)}, bf16[4,136,4]{2,1,0:T(8,128)(2,1)S(1)}, u32[]{:S(2)}, u32[]{:S(2)}) %collective-permute-start.10) | collective-permute-done | bytes 4384 | tf_op jit(solution)/shard_map/ppermute | solution.py:48
  199.5 1.9 collective-permute-start.13
  201.4 2.4 collective-permute-start.12
  203.9 2.5 collective-permute-done.12
  206.5 3.3 %collective-permute-start.15 = (bf16[4,144,8]{2,1,0:T(8,128)(2,1)S(1)}, bf16[4,144,8]{2,1,0:T(8,128)(2,1)S(1)}, u32[]{:S(2)}, u32[]{:S(2)}) collective-permute-start(bf16[4,144,8]{2,1,0:T(8,128)(2,1)S(1)} %get-tuple-element.33), channel_id=1, source_target_pairs={{2,0},{4,2},{6,4},{8,6},{10,8},{12,10},{14,12},{16,14},{18,16},{20... | collective-permute-start | bytes 27656 | tf_op jit(solution)/shard_map/ppermute | solution.py:50
  209.8 4.1 %collective-permute-start.14 = (bf16[4,144,8]{2,1,0:T(8,128)(2,1)S(1)}, bf16[4,144,8]{2,1,0:T(8,128)(2,1)S(1)}, u32[]{:S(2)}, u32[]{:S(2)}) collective-permute-start(bf16[4,144,8]{2,1,0:T(8,128)(2,1)S(1)} %get-tuple-element.32), channel_id=1, source_target_pairs={{0,2},{2,4},{4,6},{6,8},{8,10},{10,12},{12,14},{14,16},{16,18},{18... | collective-permute-start | bytes 27656 | tf_op jit(solution)/shard_map/ppermute | solution.py:48
  213.9 2.7 collective-permute-done.15
  216.6 3.7 %collective-permute-done.14 = bf16[4,144,8]{2,1,0:T(8,128)(2,1)S(1)} collective-permute-done((bf16[4,144,8]{2,1,0:T(8,128)(2,1)S(1)}, bf16[4,144,8]{2,1,0:T(8,128)(2,1)S(1)}, u32[]{:S(2)}, u32[]{:S(2)}) %collective-permute-start.14) | collective-permute-done | bytes 9248 | tf_op jit(solution)/shard_map/ppermute | solution.py:48
  221.0 0.9 fusion.21
  222.1 0.9 broadcast_in_dim.61
  222.9 3.5 %all-to-all-start.2 = ((f32[2,4,128,128]{2,1,3,0:T(4,128)}), f32[2,4,128,128]{2,1,3,0:T(4,128)S(1)}, u32[]{:S(2)}, u32[]{:S(2)}) async-start(f32[2,4,128,128]{2,1,3,0:T(4,128)} %broadcast_in_dim.61), calls=%async_computation.2 | async-start | bytes 1048576 | tf_op jit(solution)/shard_map/all_to_all | solution.py:14
  227.1 7.4 %all-to-all-done.2 = f32[2,4,128,128]{2,1,3,0:T(4,128)S(1)} async-done(((f32[2,4,128,128]{2,1,3,0:T(4,128)}), f32[2,4,128,128]{2,1,3,0:T(4,128)S(1)}, u32[]{:S(2)}, u32[]{:S(2)}) %all-to-all-start.2) | async-done | bytes 524320 | tf_op jit(solution)/shard_map/all_to_all | solution.py:14
  234.8 1.2 select_add_fusion
  236.1 0.7 fusion.104
  238.2 0.6 broadcast_multiply_fusion.4
  240.9 0.9 slice_reduce_fusion
  242.1 0.7 slice.379
  250.9 0.7 slice.401
  253.7 0.6 slice.373
  254.5 2.0 subtract_divide_fusion.2
  257.3 0.6 fusion.77
  258.7 0.7 fusion.75
  266.4 0.6 fusion.74
  267.2 1.2 subtract_divide_fusion.1
  268.5 0.7 fusion.72
  269.9 0.6 fusion.70
  271.4 0.6 fusion.68
  272.2 0.7 fusion.67
  272.9 0.7 fusion.53
  273.6 0.7 copy.146
  (164 shorter events, 24.0 us)
Async XLA Ops:
  0.0 81.9 %copy-start = (bf16[1,1,8,4,2,128,128]{6,5,4,3,2,1,0:T(8,128)(2,1)S(1)}, bf16[1,1,8,4,2,128,128]{6,5,4,3,2,1,0:T(8,128)(2,1)}, u32[]{:S(2)}) copy-start(bf16[1,1,8,4,2,128,128]{6,5,4,3,2,1,0:T(8,128)(2,1)} %param.10) | copy-start | bytes 6291460
  2.9 12.6 %copy-start.4 = (bf16[1,1,4,2,512]{4,3,2,1,0:T(2,128)(2,1)S(1)}, bf16[1,1,4,2,512]{4,3,2,1,0:T(2,128)(2,1)}, u32[]{:S(2)}) copy-start(bf16[1,1,4,2,512]{4,3,2,1,0:T(2,128)(2,1)} %param.9) | copy-start | bytes 24580
  2.9 13.2 %copy-start.3 = (s32[1,1,8,4,2]{2,4,3,1,0:T(2,128)S(1)}, s32[1,1,8,4,2]{2,4,3,1,0:T(2,128)}, u32[]{:S(2)}) copy-start(s32[1,1,8,4,2]{2,4,3,1,0:T(2,128)} %param.11) | copy-start | bytes 772
  2.9 14.7 %copy-start.6 = (s32[1,1,8]{2,1,0:T(1,128)S(1)}, s32[1,1,8]{2,1,0:T(1,128)}, u32[]{:S(2)}) copy-start(s32[1,1,8]{2,1,0:T(1,128)} %param.12) | copy-start | bytes 100
  2.9 62.2 %all-to-all-start = ((bf16[16,1,4,128,128]{4,3,2,1,0:T(8,128)(2,1)}), bf16[16,1,4,128,128]{4,3,2,1,0:T(8,128)(2,1)}, u32[]{:S(2)}, u32[]{:S(2)}) async-start(bf16[16,1,4,128,128]{4,3,2,1,0:T(8,128)(2,1)} %broadcast_in_dim.57), calls=%async_computation | async-start | bytes 4194304 | tf_op jit(solution)/shard_map/all_to_all | solution.py:14
  81.8 0.9 copy-start.2
  81.8 0.9 copy-start.8
  82.7 0.9 copy-start.7
  84.9 45.4 %all-to-all-start.1 = ((bf16[16,8,4,256]{3,2,1,0:T(4,128)(2,1)}), bf16[16,8,4,256]{3,2,1,0:T(4,128)(2,1)S(1)}, u32[]{:S(2)}, u32[]{:S(2)}) async-start(bf16[16,8,4,256]{3,2,1,0:T(4,128)(2,1)} %copy.126), calls=%async_computation.1 | async-start | bytes 524288 | tf_op jit(solution)/shard_map/all_to_all | solution.py:195
  130.1 1.7 copy-start.1
  132.4 4.3 %collective-permute-start.1 = (bf16[4,1,128]{2,1,0:T(2,128)(2,1)S(1)}, bf16[4,1,128]{2,1,0:T(2,128)(2,1)S(1)}, u32[]{:S(2)}, u32[]{:S(2)}) collective-permute-start(bf16[4,1,128]{2,1,0:T(2,128)(2,1)S(1)} %get-tuple-element.47), channel_id=1, source_target_pairs={{32,0},{64,32},{96,64},{128,96},{160,128},{192,160},{224,192},{256... | collective-permute-start | bytes 3080 | tf_op jit(solution)/shard_map/ppermute | solution.py:50
  134.3 4.9 %collective-permute-start = (bf16[4,1,128]{2,1,0:T(2,128)(2,1)S(1)}, bf16[4,1,128]{2,1,0:T(2,128)(2,1)S(1)}, u32[]{:S(2)}, u32[]{:S(2)}) collective-permute-start(bf16[4,1,128]{2,1,0:T(2,128)(2,1)S(1)} %get-tuple-element.46), channel_id=1, source_target_pairs={{0,32},{32,64},{64,96},{96,128},{128,160},{160,192},{192,224},{224... | collective-permute-start | bytes 3080 | tf_op jit(solution)/shard_map/ppermute | solution.py:48
  139.4 9.6 %collective-permute-start.3 = (bf16[4,130,1]{2,1,0:T(8,128)(2,1)S(1)}, bf16[4,130,1]{2,1,0:T(8,128)(2,1)S(1)}, u32[]{:S(2)}, u32[]{:S(2)}) collective-permute-start(bf16[4,130,1]{2,1,0:T(8,128)(2,1)S(1)} %get-tuple-element.39), channel_id=1, source_target_pairs={{2,0},{4,2},{6,4},{8,6},{10,8},{12,10},{14,12},{16,14},{18,16},{20... | collective-permute-start | bytes 3128 | tf_op jit(solution)/shard_map/ppermute | solution.py:50
  143.9 10.2 %collective-permute-start.2 = (bf16[4,130,1]{2,1,0:T(8,128)(2,1)S(1)}, bf16[4,130,1]{2,1,0:T(8,128)(2,1)S(1)}, u32[]{:S(2)}, u32[]{:S(2)}) collective-permute-start(bf16[4,130,1]{2,1,0:T(8,128)(2,1)S(1)} %get-tuple-element.38), channel_id=1, source_target_pairs={{0,2},{2,4},{4,6},{6,8},{8,10},{10,12},{12,14},{14,16},{16,18},{18... | collective-permute-start | bytes 3128 | tf_op jit(solution)/shard_map/ppermute | solution.py:48
  155.2 4.3 %collective-permute-start.5 = (bf16[4,2,128]{2,1,0:T(2,128)(2,1)S(1)}, bf16[4,2,128]{2,1,0:T(2,128)(2,1)S(1)}, u32[]{:S(2)}, u32[]{:S(2)}) collective-permute-start(bf16[4,2,128]{2,1,0:T(2,128)(2,1)S(1)} %get-tuple-element.45), channel_id=1, source_target_pairs={{32,0},{64,32},{96,64},{128,96},{160,128},{192,160},{224,192},{256... | collective-permute-start | bytes 6152 | tf_op jit(solution)/shard_map/ppermute | solution.py:50
  157.1 4.9 %collective-permute-start.4 = (bf16[4,2,128]{2,1,0:T(2,128)(2,1)S(1)}, bf16[4,2,128]{2,1,0:T(2,128)(2,1)S(1)}, u32[]{:S(2)}, u32[]{:S(2)}) collective-permute-start(bf16[4,2,128]{2,1,0:T(2,128)(2,1)S(1)} %get-tuple-element.44), channel_id=1, source_target_pairs={{0,32},{32,64},{64,96},{96,128},{128,160},{160,192},{192,224},{224... | collective-permute-start | bytes 6152 | tf_op jit(solution)/shard_map/ppermute | solution.py:48
  162.2 9.9 %collective-permute-start.7 = (bf16[4,132,2]{2,1,0:T(8,128)(2,1)S(1)}, bf16[4,132,2]{2,1,0:T(8,128)(2,1)S(1)}, u32[]{:S(2)}, u32[]{:S(2)}) collective-permute-start(bf16[4,132,2]{2,1,0:T(8,128)(2,1)S(1)} %get-tuple-element.37), channel_id=1, source_target_pairs={{2,0},{4,2},{6,4},{8,6},{10,8},{12,10},{14,12},{16,14},{18,16},{20... | collective-permute-start | bytes 6344 | tf_op jit(solution)/shard_map/ppermute | solution.py:50
  166.2 10.6 %collective-permute-start.6 = (bf16[4,132,2]{2,1,0:T(8,128)(2,1)S(1)}, bf16[4,132,2]{2,1,0:T(8,128)(2,1)S(1)}, u32[]{:S(2)}, u32[]{:S(2)}) collective-permute-start(bf16[4,132,2]{2,1,0:T(8,128)(2,1)S(1)} %get-tuple-element.36), channel_id=1, source_target_pairs={{0,2},{2,4},{4,6},{6,8},{8,10},{10,12},{12,14},{14,16},{16,18},{18... | collective-permute-start | bytes 6344 | tf_op jit(solution)/shard_map/ppermute | solution.py:48
  177.8 4.3 %collective-permute-start.9 = (bf16[4,4,128]{2,1,0:T(4,128)(2,1)S(1)}, bf16[4,4,128]{2,1,0:T(4,128)(2,1)S(1)}, u32[]{:S(2)}, u32[]{:S(2)}) collective-permute-start(bf16[4,4,128]{2,1,0:T(4,128)(2,1)S(1)} %get-tuple-element.43), channel_id=1, source_target_pairs={{32,0},{64,32},{96,64},{128,96},{160,128},{192,160},{224,192},{256... | collective-permute-start | bytes 12296 | tf_op jit(solution)/shard_map/ppermute | solution.py:50
  179.8 4.9 %collective-permute-start.8 = (bf16[4,4,128]{2,1,0:T(4,128)(2,1)S(1)}, bf16[4,4,128]{2,1,0:T(4,128)(2,1)S(1)}, u32[]{:S(2)}, u32[]{:S(2)}) collective-permute-start(bf16[4,4,128]{2,1,0:T(4,128)(2,1)S(1)} %get-tuple-element.42), channel_id=1, source_target_pairs={{0,32},{32,64},{64,96},{96,128},{128,160},{160,192},{192,224},{224... | collective-permute-start | bytes 12296 | tf_op jit(solution)/shard_map/ppermute | solution.py:48
  184.8 9.9 %collective-permute-start.11 = (bf16[4,136,4]{2,1,0:T(8,128)(2,1)S(1)}, bf16[4,136,4]{2,1,0:T(8,128)(2,1)S(1)}, u32[]{:S(2)}, u32[]{:S(2)}) collective-permute-start(bf16[4,136,4]{2,1,0:T(8,128)(2,1)S(1)} %get-tuple-element.35), channel_id=1, source_target_pairs={{2,0},{4,2},{6,4},{8,6},{10,8},{12,10},{14,12},{16,14},{18,16},{20... | collective-permute-start | bytes 13064 | tf_op jit(solution)/shard_map/ppermute | solution.py:50
  188.1 10.4 %collective-permute-start.10 = (bf16[4,136,4]{2,1,0:T(8,128)(2,1)S(1)}, bf16[4,136,4]{2,1,0:T(8,128)(2,1)S(1)}, u32[]{:S(2)}, u32[]{:S(2)}) collective-permute-start(bf16[4,136,4]{2,1,0:T(8,128)(2,1)S(1)} %get-tuple-element.34), channel_id=1, source_target_pairs={{0,2},{2,4},{4,6},{6,8},{8,10},{10,12},{12,14},{14,16},{16,18},{18... | collective-permute-start | bytes 13064 | tf_op jit(solution)/shard_map/ppermute | solution.py:48
  198.7 5.1 %copy-start.5 = (f32[4,4]{1,0:T(4,128)S(1)}, f32[4,4]{1,0:T(4,128)}, u32[]{:S(2)}) copy-start(f32[4,4]{1,0:T(4,128)} %param.14) | copy-start | bytes 196
  199.5 4.4 %collective-permute-start.13 = (bf16[4,8,128]{2,1,0:T(8,128)(2,1)S(1)}, bf16[4,8,128]{2,1,0:T(8,128)(2,1)S(1)}, u32[]{:S(2)}, u32[]{:S(2)}) collective-permute-start(bf16[4,8,128]{2,1,0:T(8,128)(2,1)S(1)} %get-tuple-element.41), channel_id=1, source_target_pairs={{32,0},{64,32},{96,64},{128,96},{160,128},{192,160},{224,192},{256... | collective-permute-start | bytes 24584 | tf_op jit(solution)/shard_map/ppermute | solution.py:50
  201.4 5.0 %collective-permute-start.12 = (bf16[4,8,128]{2,1,0:T(8,128)(2,1)S(1)}, bf16[4,8,128]{2,1,0:T(8,128)(2,1)S(1)}, u32[]{:S(2)}, u32[]{:S(2)}) collective-permute-start(bf16[4,8,128]{2,1,0:T(8,128)(2,1)S(1)} %get-tuple-element.40), channel_id=1, source_target_pairs={{0,32},{32,64},{64,96},{96,128},{128,160},{160,192},{192,224},{224... | collective-permute-start | bytes 24584 | tf_op jit(solution)/shard_map/ppermute | solution.py:48
  206.5 10.1 %collective-permute-start.15 = (bf16[4,144,8]{2,1,0:T(8,128)(2,1)S(1)}, bf16[4,144,8]{2,1,0:T(8,128)(2,1)S(1)}, u32[]{:S(2)}, u32[]{:S(2)}) collective-permute-start(bf16[4,144,8]{2,1,0:T(8,128)(2,1)S(1)} %get-tuple-element.33), channel_id=1, source_target_pairs={{2,0},{4,2},{6,4},{8,6},{10,8},{12,10},{14,12},{16,14},{18,16},{20... | collective-permute-start | bytes 27656 | tf_op jit(solution)/shard_map/ppermute | solution.py:50
  209.8 10.5 %collective-permute-start.14 = (bf16[4,144,8]{2,1,0:T(8,128)(2,1)S(1)}, bf16[4,144,8]{2,1,0:T(8,128)(2,1)S(1)}, u32[]{:S(2)}, u32[]{:S(2)}) collective-permute-start(bf16[4,144,8]{2,1,0:T(8,128)(2,1)S(1)} %get-tuple-element.32), channel_id=1, source_target_pairs={{0,2},{2,4},{4,6},{6,8},{8,10},{10,12},{12,14},{14,16},{16,18},{18... | collective-permute-start | bytes 27656 | tf_op jit(solution)/shard_map/ppermute | solution.py:48
  222.9 11.5 %all-to-all-start.2 = ((f32[2,4,128,128]{2,1,3,0:T(4,128)}), f32[2,4,128,128]{2,1,3,0:T(4,128)S(1)}, u32[]{:S(2)}, u32[]{:S(2)}) async-start(f32[2,4,128,128]{2,1,3,0:T(4,128)} %broadcast_in_dim.61), calls=%async_computation.2 | async-start | bytes 1048576 | tf_op jit(solution)/shard_map/all_to_all | solution.py:14
where the time goes:
time: 276 us; the launch traced here: 274 us
  waiting for transfers between devices  90.8 us (33%)
  starting transfers between devices  68.9 us (25%)
  blocking collectives  38.8 us (14%)
  local copies, waits for them, and re-layouts  32.8 us (12%)
  other arithmetic  19.2 us (7%)
  between operations  13 us (5%)
  matrix products  10.7 us (4%)
    all_to_all x2, waiting for transfers between devices, from_everyone(): return lax.all_to_all(copies, axis, split_axis=0, concat_axis=0, tiled=True)  53.7 us
    all_gather x1, blocking collectives, side_by_side(): filled = lax.all_gather(both, axis, axis=dim, tiled=True)  38.8 us
    ppermute x8, waiting for transfers between devices, extended(): lax.ppermute(tail, axis, [(i, (i + 1) % count) for i in range(ends)])  27.2 us
    ppermute x8, starting transfers between devices, extended(): lax.ppermute(tail, axis, [(i, (i + 1) % count) for i in range(ends)])  24.1 us
    ppermute x8, starting transfers between devices, extended(): lax.ppermute(head, axis, [((i + 1) % count, i) for i in range(ends)])  22.8 us
    all_to_all x2, starting transfers between devices, from_everyone(): return lax.all_to_all(copies, axis, split_axis=0, concat_axis=0, tiled=True)  16.1 us
    ppermute x8, waiting for transfers between devices, extended(): lax.ppermute(head, axis, [((i + 1) % count, i) for i in range(ends)])  9.98 us
    all_to_all x1, starting transfers between devices, body(): lax.all_to_all(outgoing.astype(jnp.bfloat16), 'fx', split_axis=0, concat_...  5.99 us
  transfers between devices with their start and end apart: 19, of which 14 were waited for; matrix products, arithmetic and copies ran while one was open for 1% of the time, Pallas kernels for 0%

commit v1 on v0

v1 whole, which is shorter than its diff:
```python
import functools
import math

import jax
import jax.numpy as jnp
import ml_dtypes
import numpy as np
from jax import lax
from jax.experimental import pallas as pl
from jax.experimental.pallas import tpu as pltpu
from jax.sharding import PartitionSpec as P

MESH = pl.DeviceIdType.MESH
F32 = jnp.float32
BF16 = jnp.bfloat16
STEP = 2.0


def tables(length):
    positions = np.arange(length)
    angles = (positions[:, None] * positions[None, :] % length) * (2.0 * math.pi / length)
    cosine = (np.cos(angles) / math.sqrt(length)).astype(np.float32)
    sinus = (np.sin(angles) / math.sqrt(length)).astype(np.float32)
    whole = np.concatenate(
        [np.concatenate([cosine, -sinus], axis=1), np.concatenate([sinus, cosine], axis=1)], axis=0
    )
    high = whole.astype(ml_dtypes.bfloat16)
    low = (whole - high.astype(np.float32)).astype(ml_dtypes.bfloat16)
    return np.stack([high, low])


def dot(a, b):
    return jnp.dot(a, b, preferred_element_type=F32)


def dot_nt(a, b):
    return lax.dot_general(a, b, (((1,), (1,)), ((), ())), preferred_element_type=F32)


def dot_tn(a, b):
    return lax.dot_general(a, b, (((0,), (0,)), ((), ())), preferred_element_type=F32)


def split(values):
    high = values.astype(BF16)
    return high, (values - high.astype(F32)).astype(BF16)


def dot3(a, b):
    return dot(a[0], b[0]) + (dot(a[0], b[1]) + dot(a[1], b[0]))


def kernel(
    sizes,
    sky_hbm,
    vis_hbm,
    w_hbm,
    tiles_s,
    list_s,
    count_s,
    thr_s,
    mu_s,
    tab_hbm,
    out_ref,
    sky_v,
    vis_v,
    wv,
    tab,
    idx_send,
    idx_recv,
    spec,
    row_send,
    row_recv,
    con_buf,
    con_send,
    con_recv,
    inv_s,
    st_bf,
    edge_send,
    top_recv,
    bot_recv,
    vl,
    vr,
    ext,
    pa,
    pb,
    shr,
    shr_send,
    shr_recv,
    gpart,
    gtot,
    xs,
    local_sem,
    idx_ssem,
    idx_rsem,
    row_ssem,
    row_rsem,
    con_ssem,
    con_rsem,
    halo_ssem,
    halo_rsem,
    blk_ssem,
    blk_rsem,
):
    nfx, nfy, nblk, fpb, vt, nnz = sizes
    n_chan, size, _ = sky_v.shape
    slots = vt * nnz
    lanes = nfx * 2 * slots
    fy, fx, blk = lax.axis_index("fy"), lax.axis_index("fx"), lax.axis_index("blk")

    def along_fx(d):
        return (fy, lax.rem(fx + d, nfx), blk)

    up, down = lax.rem(fy + nfy - 1, nfy), lax.rem(fy + 1, nfy)
    left, right = lax.rem(fx + nfx - 1, nfx), lax.rem(fx + 1, nfx)
    mate = (fy, fx, 1 - blk)

    loads = []

    def load(src, dst):
        copy = pltpu.make_async_copy(src, dst, local_sem.at[len(loads)])
        copy.start()
        loads.append(copy)
        return copy

    tab_load = load(tab_hbm, tab)
    sky_load = load(sky_hbm, sky_v)
    vis_load = load(vis_hbm, vis_v)
    w_loads = [
        load(w_hbm.at[f, :, n], wv.at[f // 2, n, :, :, pl.ds((f % 2) * size, size)])
        for f in range(fpb)
        for n in range(nnz)
    ]

    barrier = pltpu.get_barrier_semaphore()
    others = [along_fx(d) for d in range(1, nfx)]
    others += [(up, fx, blk), (down, fx, blk), mate]
    others += [(r, c, blk) for r in (up, down) for c in (left, right)]
    for device in others:
        pl.semaphore_signal(barrier, inc=1, device_id=device, device_id_type=MESH)

    lane = lax.broadcasted_iota(jnp.int32, (1, lanes), 1)
    lane_a, lane_n = lane % vt, (lane // vt) % nnz
    lane_p, lane_j = (lane // slots) % 2, lane // (2 * slots)
    wanted = []
    for f in range(fpb):
        row = jnp.zeros((1, lanes), jnp.int32)
        for a in range(vt):
            for n in range(nnz):
                here = (lane_a == a) & (lane_n == n)
                row = jnp.where(here, tiles_s[(f * vt + a) * nnz + n], row)
        wanted.append(jnp.where(lane_j == fx, row + lane_p * size + 1, 0))
    for k in range(nfx):
        request = jnp.zeros((1, lanes), jnp.int32)
        place = fpb
        for f in range(fpb):
            hit = list_s[f] == k
            request = jnp.where(hit, wanted[f], request)
            place = jnp.where(hit, f, place)
        idx_send[k] = request
        inv_s[k] = place
    idx_recv[fx] = idx_send[fx]

    pl.semaphore_wait(barrier, len(others))

    order = sorted(range(1, nfx), key=lambda d: -min(d, nfx - d))

    def exchange(send, recv, ssem, rsem):
        copies = []
        for d in order:
            copy = pltpu.make_async_remote_copy(
                src_ref=send.at[lax.rem(fx + d, nfx)],
                dst_ref=recv.at[fx],
                send_sem=ssem.at[d],
                recv_sem=rsem.at[d],
                device_id=along_fx(d),
                device_id_type=MESH,
            )
            copy.start()
            copies.append(copy)
        return copies

    pending = exchange(idx_send, idx_recv, idx_ssem, idx_rsem)
    idx_copies = pending

    tab_load.wait()
    sky_load.wait()
    high = tab[0]
    left_table = jnp.concatenate([high[:size, :size], high[:size, size:]], axis=0)
    for c in range(n_chan):
        half = dot(left_table, sky_v[c]).astype(BF16)
        half = jnp.concatenate([half[:size], half[size:]], axis=1)
        full = dot(half, high).astype(BF16)
        spec[:size, c * size : (c + 1) * size] = full[:, :size]
        spec[size:, c * size : (c + 1) * size] = full[:, size:]

    for copy in idx_copies:
        copy.wait_recv()
    target = jnp.sum(idx_recv[...], axis=0)
    row_ids = lax.broadcasted_iota(jnp.int32, (2 * size, lanes), 0) + 1
    place_mat = jnp.where(row_ids == target, 1.0, 0.0).astype(BF16)
    group = 2 * slots
    for c in range(n_chan):
        picked = dot_tn(place_mat, spec[:, c * size : (c + 1) * size])
        row_send[:, c * group : (c + 1) * group, :] = picked.reshape(nfx, group, size).astype(BF16)
    row_recv[fx] = row_send[fx]
    row_copies = exchange(row_send, row_recv, row_ssem, row_rsem)

    rows_all = n_chan * 2 * slots
    n_vis = vt * size
    vis_load.wait()
    row_id = lax.broadcasted_iota(jnp.int32, (rows_all, n_vis), 0)
    vis_id = lax.broadcasted_iota(jnp.int32, (rows_all, n_vis), 1)
    live = (vis_id < count_s[0]) & (row_id % vt == vis_id // size)
    first_slot = (row_id // vt) % nnz == 0
    measured = []
    for c in range(n_chan):
        both = vis_v[c].astype(F32)
        for p in range(2):
            measured.append(jnp.broadcast_to(both[p : p + 1], (slots, n_vis)))
    measured = jnp.concatenate(measured, axis=0)
    con_buf[fpb] = jnp.zeros((rows_all, size), BF16)
    for copy in w_loads:
        copy.wait()
    for copy in row_copies:
        copy.wait_recv()

    sums = [None, None]
    for q in range(fpb // 2):
        x = jnp.concatenate([row_recv[list_s[2 * q]], row_recv[list_s[2 * q + 1]]], axis=1)
        for n in range(nnz):
            term = dot_nt(x, wv[q, n].reshape(n_vis, 2 * size))
            sums[n] = term if sums[n] is None else sums[n] + term
    mixed = jnp.where(first_slot, sums[0], sums[1])
    later = pltpu.roll(mixed, rows_all - vt, 0)
    earlier = pltpu.roll(mixed, vt, 0)
    predicted = mixed + jnp.where(first_slot, later, earlier)
    residual = jnp.where(live, predicted - measured, 0.0).astype(BF16)
    first_out = (lax.broadcasted_iota(jnp.int32, (rows_all, 2 * size), 0) // vt) % nnz == 0
    for q in range(fpb // 2):
        terms = [dot(residual, wv[q, n].reshape(n_vis, 2 * size)) for n in range(nnz)]
        out = jnp.where(first_out, terms[0], terms[1]).astype(BF16)
        con_buf[2 * q] = out[:, :size]
        con_buf[2 * q + 1] = out[:, size:]
    for k in range(nfx):
        con_send[k] = con_buf[inv_s[k]]
    con_recv[fx] = con_send[fx]
    con_copies = exchange(con_send, con_recv, con_ssem, con_rsem)

    def flipped(table):
        return jnp.concatenate(
            [
                jnp.concatenate([table[:size, :size], table[size:, :size]], axis=1),
                jnp.concatenate([table[:size, size:], table[size:, size:]], axis=1),
            ],
            axis=0,
        )

    for copy in con_copies:
        copy.wait_recv()
    right_back = (flipped(tab[0]), flipped(tab[1]))
    left_back = (tab[0, :size, :], tab[1, :size, :])
    edge = jnp.zeros((size, size), F32)
    lane_c = lax.broadcasted_iota(jnp.int32, (size, size), 1) // 32
    for c in range(n_chan):
        incoming = con_recv[:, c * group : (c + 1) * group, :].reshape(nfx * group, size)
        own = dot(place_mat, incoming)
        own = jnp.concatenate([own[:size], own[size:]], axis=1)
        half = dot3(split(own), right_back)
        half = jnp.concatenate([half[:, :size], half[:, size:]], axis=0)
        grad = dot3(left_back, split(half))
        stepped = sky_v[c].astype(F32) - STEP * grad
        ext[c, 0, 24 : 24 + size, :] = stepped
        shr[c] = stepped
        st_bf[c] = stepped.astype(BF16)
        edge = jnp.where(lane_c == c, pltpu.roll(stepped, 16 + 32 * c, 1), edge)
    edge_send[...] = edge.astype(BF16)

    last = size - 16
    halo = [
        (st_bf.at[:, pl.ds(0, 16), :], bot_recv, (up, fx, blk)),
        (st_bf.at[:, pl.ds(last, 16), :], top_recv, (down, fx, blk)),
        (edge_send, vr.at[pl.ds(16, size), :], (fy, left, blk)),
        (edge_send, vl.at[pl.ds(16, size), :], (fy, right, blk)),
        (edge_send.at[pl.ds(0, 16), :], vr.at[pl.ds(16 + size, 16), :], (up, left, blk)),
        (edge_send.at[pl.ds(0, 16), :], vl.at[pl.ds(16 + size, 16), :], (up, right, blk)),
        (edge_send.at[pl.ds(last, 16), :], vr.at[pl.ds(0, 16), :], (down, left, blk)),
        (edge_send.at[pl.ds(last, 16), :], vl.at[pl.ds(0, 16), :], (down, right, blk)),
    ]
    halo_copies = []
    for h in (4, 5, 6, 7, 2, 3, 0, 1):
        src, dst, device = halo[h]
        copy = pltpu.make_async_remote_copy(
            src_ref=src,
            dst_ref=dst,
            send_sem=halo_ssem.at[h],
            recv_sem=halo_rsem.at[h],
            device_id=device,
            device_id_type=MESH,
        )
        copy.start()
        halo_copies.append(copy)

    tall = size + 32
    in_top, in_bottom = fy > 0, fy < nfy - 1
    in_left, in_right = fx > 0, fx < nfx - 1
    lane_id = lax.broadcasted_iota(jnp.int32, (1, size), 1)
    side_live = ((lane_id < 64) & in_right) | ((lane_id >= 64) & in_left)
    row_tall = lax.broadcasted_iota(jnp.int32, (tall, 1), 0)
    rows_live = ((row_tall >= 16) | in_top) & ((row_tall < 16 + size) | in_bottom)
    wide_live = rows_live & side_live

    for copy in halo_copies:
        copy.wait_recv()
    from_left = vl[...].astype(F32)
    from_right = vr[...].astype(F32)
    zeros8 = jnp.zeros((8, size), F32)
    for c in range(n_chan):
        ext[c, 0, 8:24, :] = jnp.where(in_top, top_recv[c].astype(F32), 0.0)
        ext[c, 0, 24 + size : 40 + size, :] = jnp.where(in_bottom, bot_recv[c].astype(F32), 0.0)
        r = pltpu.roll(from_right, (size - (32 * c + 16)) % size, 1)
        l = pltpu.roll(from_left, (size - 16 - 32 * c) % size, 1)
        side = jnp.where(lane_id < 16, r, jnp.where(lane_id >= size - 16, l, 0.0))
        ext[c, 1, 8 : 8 + tall, :] = jnp.where(wide_live, side, 0.0)
        for t in range(2):
            ext[c, t, 0:8, :] = zeros8
            ext[c, t, 8 + tall : 16 + tall, :] = zeros8
    for buf in (pa, pb):
        for t in range(2):
            buf[t, 0:8, :] = zeros8
            buf[t, 8 + tall : 16 + tall, :] = zeros8

    spans = [(8, 8 + tall, 32), (8, 8 + tall, 32), (16, tall, 48), (24, 24 + size, 32)]
    blk_copies = []
    for c in range(n_chan):
        source = ext.at[c]
        for level in range(len(spans)):
            s = 2**level
            low, top, chunk = spans[level]
            final = level == len(spans) - 1
            dest = None if final else (pa, pb)[level % 2]
            bound = thr_s[level, c]
            for at in range(low, top, chunk):
                tiles = []
                for t in range(2):
                    tiles.append(
                        (
                            source[t, at - s : at - s + chunk, :]
                            + 2.0 * source[t, at : at + chunk, :]
                            + source[t, at + s : at + s + chunk, :]
                        )
                        * 0.25
                    )
                rr = [pltpu.roll(v, s, 1) for v in tiles]
                ll = [pltpu.roll(v, size - s, 1) for v in tiles]
                lo_lane, hi_lane = lane_id < s, lane_id >= size - s
                smooth = (
                    jnp.where(lo_lane, rr[1], rr[0])
                    + 2.0 * tiles[0]
                    + jnp.where(hi_lane, ll[1], ll[0])
                ) * 0.25
                if not final:
                    side = (
                        jnp.where(lo_lane, rr[0], rr[1])
                        + 2.0 * tiles[1]
                        + jnp.where(hi_lane, ll[0], ll[1])
                    ) * 0.25
                    inside = rows_live[at - 8 : at - 8 + chunk]
                    if at < 24 or at + chunk > 24 + size:
                        smooth = jnp.where(inside, smooth, 0.0)
                        side = jnp.where(inside & side_live, side, 0.0)
                    else:
                        side = jnp.where(side_live, side, 0.0)
                    dest[0, at : at + chunk, :] = smooth
                    dest[1, at : at + chunk, :] = side
                first, stop = max(at, 24), min(at + chunk, 24 + size)
                detail = source[0, first:stop, :] - smooth[first - at : stop - at]
                own_rows = slice(first - 24, stop - 24)
                shr[c, own_rows, :] = shr[c, own_rows, :] - jnp.clip(detail, -bound, bound)
            source = dest
        shr_send[c] = shr[c].astype(BF16)
        copy = pltpu.make_async_remote_copy(
            src_ref=shr_send.at[c],
            dst_ref=shr_recv.at[c],
            send_sem=blk_ssem.at[c],
            recv_sem=blk_rsem.at[c],
            device_id=mate,
            device_id_type=MESH,
        )
        copy.start()
        blk_copies.append(copy)

    total = 2 * n_chan
    chunk = 16

    def products(pairs, first):
        def step(i, sums):
            rows = pl.ds(pl.multiple_of(i * chunk, chunk), chunk)
            vals = [shr[c, rows, :] for c in range(n_chan)]
            if not first:
                vals += [shr_recv[c, rows, :].astype(F32) for c in range(n_chan)]
            news = []
            for k, (a, b) in enumerate(pairs):
                prod = vals[a] * vals[b]
                news.append(sums[k] + (prod[:8] + prod[8:]))
            return tuple(news)

        start = tuple(jnp.zeros((8, size), F32) for _ in pairs)
        sums = lax.fori_loop(0, size // chunk, step, start)
        for (a, b), value in zip(pairs, sums):
            value = jnp.sum(value, axis=0, keepdims=True)
            gpart[a * total + b : a * total + b + 1, :] = value
            if a != b:
                gpart[b * total + a : b * total + a + 1, :] = value

    everyone = [(a, b) for a in range(total) for b in range(a, total)]
    products([(a, b) for a, b in everyone if b < n_chan], True)
    for copy in blk_copies:
        copy.wait_recv()
    products([(a, b) for a, b in everyone if b >= n_chan], False)
    gtot[...] = jnp.broadcast_to(jnp.sum(gpart[...], axis=1, keepdims=True), gtot.shape)

    mu = mu_s[0] * float(size * size)
    mat = {}
    for a, b in everyone:
        value = jnp.broadcast_to(gtot[a * total + b : a * total + b + 1, :], (total, size))
        mat[a, b] = value + mu if a == b else value
    rhs = [gtot[c * total : (c + 1) * total, :] for c in range(total)]
    inverse = [None] * total
    for k in range(total):
        inverse[k] = 1.0 / mat[k, k]
        for i in range(k + 1, total):
            factor = mat[k, i] * inverse[k]
            for j in range(i, total):
                mat[i, j] = mat[i, j] - factor * mat[k, j]
            rhs[i] = rhs[i] - factor * rhs[k]
    solved = [None] * total
    for k in range(total - 1, -1, -1):
        value = rhs[k]
        for i in range(k + 1, total):
            value = value - mat[k, i] * solved[i]
        solved[k] = value * inverse[k]
        xs[k * total : (k + 1) * total, :] = solved[k]

    coeffs = [
        [jnp.broadcast_to(xs[c * total + d : c * total + d + 1, :], (8, size)) for c in range(total)]
        for d in range(n_chan)
    ]

    def finish(i, carry):
        rows = pl.ds(pl.multiple_of(i * chunk, chunk), chunk)
        vals = [shr[c, rows, :] for c in range(n_chan)]
        vals += [shr_recv[c, rows, :].astype(F32) for c in range(n_chan)]
        for d in range(n_chan):
            for h in range(2):
                value = coeffs[d][0] * vals[0][h * 8 : h * 8 + 8]
                for c in range(1, total):
                    value = value + coeffs[d][c] * vals[c][h * 8 : h * 8 + 8]
                out_ref[d, pl.ds(pl.multiple_of(i * chunk + h * 8, 8), 8), :] = value
        return carry

    lax.fori_loop(0, size // chunk, finish, 0)

    for copy in idx_copies + row_copies + con_copies + halo_copies + blk_copies:
        copy.wait_send()


def body(sizes, sky, vis, weights, tiles, lists, count, threshold, weight):
    nfx, nfy, nblk, fpb, vt, nnz = sizes
    n_chan, size, _ = sky.shape
    rows = n_chan * 2 * vt * nnz
    lanes = nfx * 2 * vt * nnz
    hbm = pl.BlockSpec(memory_space=pl.ANY)
    smem = pl.BlockSpec(memory_space=pltpu.SMEM)
    tall = size + 48
    sem = pltpu.SemaphoreType.DMA
    return pl.pallas_call(
        functools.partial(kernel, sizes),
        out_shape=jax.ShapeDtypeStruct((n_chan, size, size), F32),
        in_specs=[hbm, hbm, hbm, smem, smem, smem, smem, smem, hbm],
        out_specs=pl.BlockSpec(memory_space=pltpu.VMEM),
        scratch_shapes=[
            pltpu.VMEM((n_chan, size, size), BF16),
            pltpu.VMEM((n_chan, 2, vt * size), BF16),
            pltpu.VMEM((fpb // 2, nnz, vt, size, 2 * size), BF16),
            pltpu.VMEM((2, 2 * size, 2 * size), BF16),
            pltpu.VMEM((nfx, 1, lanes), jnp.int32),
            pltpu.VMEM((nfx, 1, lanes), jnp.int32),
            pltpu.VMEM((2 * size, n_chan * size), BF16),
            pltpu.VMEM((nfx, rows, size), BF16),
            pltpu.VMEM((nfx, rows, size), BF16),
            pltpu.VMEM((fpb + 1, rows, size), BF16),
            pltpu.VMEM((nfx, rows, size), BF16),
            pltpu.VMEM((nfx, rows, size), BF16),
            pltpu.SMEM((nfx,), jnp.int32),
            pltpu.VMEM((n_chan, size, size), BF16),
            pltpu.VMEM((size, size), BF16),
            pltpu.VMEM((n_chan, 16, size), BF16),
            pltpu.VMEM((n_chan, 16, size), BF16),
            pltpu.VMEM((size + 32, size), BF16),
            pltpu.VMEM((size + 32, size), BF16),
            pltpu.VMEM((n_chan, 2, tall, size), F32),
            pltpu.VMEM((2, tall, size), F32),
            pltpu.VMEM((2, tall, size), F32),
            pltpu.VMEM((n_chan, size, size), F32),
            pltpu.VMEM((n_chan, size, size), BF16),
            pltpu.VMEM((n_chan, size, size), BF16),
            pltpu.VMEM((4 * n_chan * n_chan, size), F32),
            pltpu.VMEM((4 * n_chan * n_chan, size), F32),
            pltpu.VMEM((4 * n_chan * n_chan, size), F32),
            sem((3 + fpb * nnz,)),
            sem((nfx,)),
            sem((nfx,)),
            sem((nfx,)),
            sem((nfx,)),
            sem((nfx,)),
            sem((nfx,)),
            sem((8,)),
            sem((8,)),
            sem((n_chan,)),
            sem((n_chan,)),
        ],
        compiler_params=pltpu.CompilerParams(collective_id=0, has_side_effects=True),
    )(
        sky,
        vis[0, 0],
        weights[0, 0],
        tiles.reshape(-1),
        lists.reshape(-1),
        count.reshape(-1),
        threshold,
        weight.reshape(1),
        jnp.asarray(tables(size)),
    )


def solution(mesh):
    in_specs = (
        P("blk", "fy", "fx"),
        P("fy", "fx", "blk", None, None),
        P("fy", "fx", None, None, None, None, None),
        P("fy", "fx", None, None, None),
        P("fy", "fx", None),
        P("fy", "fx"),
        P(None, "blk"),
        P(),
    )

    def step(*args):
        fpb, vt, nnz = args[3].shape[2:]
        sizes = (mesh.shape["fx"], mesh.shape["fy"], mesh.shape["blk"], fpb, vt, nnz)
        return body(sizes, *args)

    return jax.shard_map(
        step, mesh=mesh, in_specs=in_specs, out_specs=P("blk", "fy", "fx"), check_vma=False
    )
```

time: 276 us -> 58.4 us (0.21)
  the two profiles are of different devices: /device:TPU:88 before, /device:TPU:1 now
where the time goes in v1:
time: 58.4 us; the launch traced here: 57.4 us
  Pallas kernels  53 us (91%)
  local copies, waits for them, and re-layouts  3.08 us (5%)
  between operations  1.31 us (2%)
    pallas_call x1, Pallas kernels, body(): pl.pallas_call(functools.partial(kernel, sizes), out_shape=jax.ShapeDtype...  53 us
    unnamed x2, local copies, waits for them, and re-layouts  2.46 us

profile of v1, /device:TPU:1, one launch (start us, length us, event | category | flops | bytes accessed | tf_op | source)
XLA Modules:
  0.0 57.4 jit_solution(3906159354126998076)
XLA Ops:
  1.3 0.8 %copy.11 = s32[1,1,8,4,2]{4,3,2,1,0:T(4,128)S(1)} copy(s32[1,1,8,4,2]{2,4,3,1,0:T(2,128)} %param.12) | data formatting | bytes 512 | tf_op args[3]
  2.1 0.6 %reshape.12.tiles_s = s32[64]{0:T(128)} reshape(s32[1,1,8,4,2]{4,3,2,1,0:T(4,128)S(1)} %copy.11) | data formatting | bytes 512 | tf_op jit(solution)/shard_map/reshape | solution.py:528
  2.7 53.0 %shard_map.91 = f32[4,128,128]{2,1,0:T(8,128)} custom-call(bf16[4,128,128]{2,1,0:T(8,128)(2,1)} %sky_hbm.1, bf16[4,2,512]{2,1,0:T(2,128)(2,1)} %bitcast.8, bf16[8,4,2,128,128]{4,3,2,1,0:T(8,128)(2,1)} %bitcast.7, s32[64]{0:T(128)} %reshape.12.tiles_s, s32[8]{0:T(128)} %bitcast.9, s32[1]{0:T(128)} %bitcast.5.count_s, f32[4,4]{1,0:T(4,128)} %thr_s.1, ...), custom_call_target="tpu_custom_call" | custom-call | tf_op jit(solution)/shard_map/pallas_call | solution.py:477
  55.8 1.7 %copy.15 = f32[4,128,128]{2,1,0:T(8,128)} copy(f32[4,128,128]{2,1,0:T(8,128)} %shard_map.91) | data formatting | bytes 524288

commit v2 on v1

v2 whole, which is shorter than its diff:
```python
import functools
import math

import jax
import jax.numpy as jnp
import ml_dtypes
import numpy as np
from jax import lax
from jax.experimental import pallas as pl
from jax.experimental.pallas import tpu as pltpu
from jax.sharding import PartitionSpec as P

MESH = pl.DeviceIdType.MESH
F32 = jnp.float32
BF16 = jnp.bfloat16
STEP = 2.0


def tables(length):
    positions = np.arange(length)
    angles = (positions[:, None] * positions[None, :] % length) * (2.0 * math.pi / length)
    cosine = (np.cos(angles) / math.sqrt(length)).astype(np.float32)
    sinus = (np.sin(angles) / math.sqrt(length)).astype(np.float32)
    whole = np.concatenate(
        [np.concatenate([cosine, -sinus], axis=1), np.concatenate([sinus, cosine], axis=1)], axis=0
    )
    high = whole.astype(ml_dtypes.bfloat16)
    low = (whole - high.astype(np.float32)).astype(ml_dtypes.bfloat16)
    return np.stack([high, low])


def dot(a, b):
    return jnp.dot(a, b, preferred_element_type=F32)


def dot_nt(a, b):
    return lax.dot_general(a, b, (((1,), (1,)), ((), ())), preferred_element_type=F32)


def dot_tn(a, b):
    return lax.dot_general(a, b, (((0,), (0,)), ((), ())), preferred_element_type=F32)


def split(values):
    high = values.astype(BF16)
    return high, (values - high.astype(F32)).astype(BF16)


def dot3(a, b):
    return dot(a[0], b[0]) + (dot(a[0], b[1]) + dot(a[1], b[0]))


def pinned(array):
    return pltpu.with_memory_space_constraint(array, pltpu.HBM)


def kernel(
    sizes,
    sky_hbm,
    vis_hbm,
    w_hbm,
    tiles_hbm,
    list_hbm,
    count_s,
    thr_hbm,
    tab_hbm,
    shr,
    other,
    tiles_s,
    list_s,
    thr_s,
    sky_v,
    vis_v,
    wv,
    tab,
    idx_send,
    idx_recv,
    spec,
    row_send,
    row_recv0,
    row_recv1,
    con_buf,
    con_send,
    con_recv,
    inv_s,
    st_bf,
    edge_send,
    top_recv,
    bot_recv,
    vl,
    vr,
    ext,
    pa,
    pb,
    shr_send,
    shr_recv,
    local_sem,
    idx_ssem,
    idx_rsem,
    row_ssem,
    row_rsem,
    con_ssem,
    con_rsem,
    halo_ssem,
    halo_rsem,
    blk_ssem,
    blk_rsem,
):
    nfx, nfy, nblk, fpb, vt, nnz, halves = sizes
    n_chan, size, _ = sky_v.shape
    per = n_chan // halves
    row_recv = (row_recv0, row_recv1)
    slots = vt * nnz
    lanes = nfx * 2 * slots
    fy, fx, blk = lax.axis_index("fy"), lax.axis_index("fx"), lax.axis_index("blk")

    def along_fx(d):
        return (fy, lax.rem(fx + d, nfx), blk)

    up, down = lax.rem(fy + nfy - 1, nfy), lax.rem(fy + 1, nfy)
    left, right = lax.rem(fx + nfx - 1, nfx), lax.rem(fx + 1, nfx)
    mate = (fy, fx, 1 - blk)

    loads = []

    def load(src, dst):
        copy = pltpu.make_async_copy(src, dst, local_sem.at[len(loads)])
        copy.start()
        loads.append(copy)
        return copy

    barrier = pltpu.get_barrier_semaphore()
    others = [along_fx(d) for d in range(1, nfx)]
    others += [(up, fx, blk), (down, fx, blk), mate]
    others += [(r, c, blk) for r in (up, down) for c in (left, right)]
    for device in others:
        pl.semaphore_signal(barrier, inc=1, device_id=device, device_id_type=MESH)

    small_loads = [
        load(tiles_hbm, tiles_s),
        load(list_hbm, list_s),
        load(thr_hbm, thr_s),
    ]
    tab_load = load(tab_hbm, tab)
    sky_load = load(sky_hbm, sky_v)
    vis_load = load(vis_hbm, vis_v)
    w_loads = [
        load(w_hbm.at[f, :, n], wv.at[f // 2, n, :, :, pl.ds((f % 2) * size, size)])
        for f in range(fpb)
        for n in range(nnz)
    ]

    for copy in small_loads:
        copy.wait()
    lane = lax.broadcasted_iota(jnp.int32, (1, lanes), 1)
    lane_a, lane_n = lane % vt, (lane // vt) % nnz
    lane_p, lane_j = (lane // slots) % 2, lane // (2 * slots)
    wanted = []
    for f in range(fpb):
        row = jnp.zeros((1, lanes), jnp.int32)
        for a in range(vt):
            for n in range(nnz):
                here = (lane_a == a) & (lane_n == n)
                row = jnp.where(here, tiles_s[a, n, f], row)
        wanted.append(jnp.where(lane_j == fx, row + lane_p * size + 1, 0))
    for k in range(nfx):
        request = jnp.zeros((1, lanes), jnp.int32)
        place = fpb
        for f in range(fpb):
            hit = list_s[f] == k
            request = jnp.where(hit, wanted[f], request)
            place = jnp.where(hit, f, place)
        idx_send[k] = request
        inv_s[k] = place
    idx_recv[fx] = idx_send[fx]

    pl.semaphore_wait(barrier, len(others))

    order = sorted(range(1, nfx), key=lambda d: -min(d, nfx - d))

    def exchange(send, recv, ssem, rsem):
        copies = []
        for d in order:
            copy = pltpu.make_async_remote_copy(
                src_ref=send.at[lax.rem(fx + d, nfx)],
                dst_ref=recv.at[fx],
                send_sem=ssem.at[d],
                recv_sem=rsem.at[d],
                device_id=along_fx(d),
                device_id_type=MESH,
            )
            copy.start()
            copies.append(copy)
        return copies

    idx_copies = exchange(idx_send, idx_recv, idx_ssem, idx_rsem)

    tab_load.wait()
    sky_load.wait()
    high = tab[0]
    left_table = jnp.concatenate([high[:size, :size], high[:size, size:]], axis=0)
    for c in range(n_chan):
        half = dot(left_table, sky_v[c]).astype(BF16)
        half = jnp.concatenate([half[:size], half[size:]], axis=1)
        full = dot(half, high).astype(BF16)
        spec[:size, c * size : (c + 1) * size] = full[:, :size]
        spec[size:, c * size : (c + 1) * size] = full[:, size:]

    for copy in idx_copies:
        copy.wait_recv()
    target = jnp.sum(idx_recv[...], axis=0)
    row_ids = lax.broadcasted_iota(jnp.int32, (2 * size, lanes), 0) + 1
    place_mat = jnp.where(row_ids == target, 1.0, 0.0).astype(BF16)
    group = 2 * slots
    row_copies = []
    for h in range(halves):
        span = slice(h * per * size, (h + 1) * per * size)
        picked = dot_tn(place_mat, spec[:, span]).astype(BF16)
        for c in range(per):
            row_send[h, :, c * group : (c + 1) * group, :] = picked[
                :, c * size : (c + 1) * size
            ].reshape(nfx, group, size)
        row_recv[h][fx] = row_send[h, fx]
        row_copies.append(
            exchange(row_send.at[h], row_recv[h], row_ssem.at[h], row_rsem.at[h])
        )

    rows_all = per * group
    n_vis = vt * size
    vis_load.wait()
    row_id = lax.broadcasted_iota(jnp.int32, (rows_all, n_vis), 0)
    vis_id = lax.broadcasted_iota(jnp.int32, (rows_all, n_vis), 1)
    live = (vis_id < count_s[0]) & (row_id % vt == vis_id // size)
    first_slot = (row_id // vt) % nnz == 0
    first_out = (lax.broadcasted_iota(jnp.int32, (rows_all, 2 * size), 0) // vt) % nnz == 0
    for h in range(halves):
        con_buf[h, fpb] = jnp.zeros((rows_all, size), BF16)
    for copy in w_loads:
        copy.wait()

    con_copies = []
    for h in range(halves):
        for copy in row_copies[h]:
            copy.wait_recv()
        measured = []
        for c in range(per):
            both = vis_v[h * per + c].astype(F32)
            for p in range(2):
                measured.append(jnp.broadcast_to(both[p : p + 1], (slots, n_vis)))
        measured = jnp.concatenate(measured, axis=0)
        sums = [None, None]
        for q in range(fpb // 2):
            x = jnp.concatenate(
                [row_recv[h][list_s[2 * q]], row_recv[h][list_s[2 * q + 1]]], axis=1
            )
            for n in range(nnz):
                term = dot_nt(x, wv[q, n].reshape(n_vis, 2 * size))
                sums[n] = term if sums[n] is None else sums[n] + term
        mixed = jnp.where(first_slot, sums[0], sums[1])
        later = pltpu.roll(mixed, rows_all - vt, 0)
        earlier = pltpu.roll(mixed, vt, 0)
        predicted = mixed + jnp.where(first_slot, later, earlier)
        residual = jnp.where(live, predicted - measured, 0.0).astype(BF16)
        for q in range(fpb // 2):
            terms = [dot(residual, wv[q, n].reshape(n_vis, 2 * size)) for n in range(nnz)]
            out = jnp.where(first_out, terms[0], terms[1]).astype(BF16)
            con_buf[h, 2 * q] = out[:, :size]
            con_buf[h, 2 * q + 1] = out[:, size:]
        for k in range(nfx):
            con_send[h, k] = con_buf[h, inv_s[k]]
        con_recv[h, fx] = con_send[h, fx]
        con_copies.append(
            exchange(con_send.at[h], con_recv.at[h], con_ssem.at[h], con_rsem.at[h])
        )

    def flipped(table):
        return jnp.concatenate(
            [
                jnp.concatenate([table[:size, :size], table[size:, :size]], axis=1),
                jnp.concatenate([table[:size, size:], table[size:, size:]], axis=1),
            ],
            axis=0,
        )

    right_back = (flipped(tab[0]), flipped(tab[1]))
    left_back = (tab[0, :size, :], tab[1, :size, :])
    lane_id = lax.broadcasted_iota(jnp.int32, (1, size), 1)
    mid = size // 2
    halo_copies = []
    for h in range(halves):
        for copy in con_copies[h]:
            copy.wait_recv()
        incoming = jnp.concatenate(
            [
                con_recv[h, :, c * group : (c + 1) * group, :].reshape(nfx * group, size)
                for c in range(per)
            ],
            axis=1,
        )
        own = dot(place_mat, incoming)
        own = jnp.concatenate(
            [
                jnp.concatenate(
                    [own[:size, c * size : (c + 1) * size], own[size:, c * size : (c + 1) * size]],
                    axis=1,
                )
                for c in range(per)
            ],
            axis=0,
        )
        half = dot3(split(own), right_back)
        half = jnp.concatenate(
            [
                jnp.concatenate(
                    [half[c * size : (c + 1) * size, :size], half[c * size : (c + 1) * size, size:]],
                    axis=0,
                )
                for c in range(per)
            ],
            axis=1,
        )
        grad = dot3(left_back, split(half))
        edge = jnp.zeros((mid, size), F32)
        for c in range(per):
            stepped = sky_v[h * per + c].astype(F32) - STEP * grad[:, c * size : (c + 1) * size]
            ext[h * per + c, 0, 24 : 24 + size, :] = stepped
            shr[h * per + c] = stepped
            st_bf[h, c] = stepped.astype(BF16)
            for fold in range(2):
                at = fold * mid + 32 * c
                part = pltpu.roll(stepped[fold * mid : (fold + 1) * mid], (16 + at) % size, 1)
                edge = jnp.where((lane_id >= at) & (lane_id < at + 32), part, edge)
        edge_send[h] = edge.astype(BF16)

        first, last = pl.ds(0, 16), pl.ds(mid - 16, 16)
        main, low = pl.ds(16, mid), pl.ds(16 + mid, 16)
        halo = [
            (edge_send.at[h, first], vr.at[h, low], (up, left, blk)),
            (edge_send.at[h, first], vl.at[h, low], (up, right, blk)),
            (edge_send.at[h, last], vr.at[h, first], (down, left, blk)),
            (edge_send.at[h, last], vl.at[h, first], (down, right, blk)),
            (edge_send.at[h], vr.at[h, main], (fy, left, blk)),
            (edge_send.at[h], vl.at[h, main], (fy, right, blk)),
            (st_bf.at[h, :, pl.ds(0, 16), :], bot_recv.at[h], (up, fx, blk)),
            (st_bf.at[h, :, pl.ds(size - 16, 16), :], top_recv.at[h], (down, fx, blk)),
        ]
        copies = []
        for k, (src, dst, device) in enumerate(halo):
            copy = pltpu.make_async_remote_copy(
                src_ref=src,
                dst_ref=dst,
                send_sem=halo_ssem.at[h, k],
                recv_sem=halo_rsem.at[h, k],
                device_id=device,
                device_id_type=MESH,
            )
            copy.start()
            copies.append(copy)
        halo_copies.append(copies)

    tall = size + 32
    in_top, in_bottom = fy > 0, fy < nfy - 1
    in_left, in_right = fx > 0, fx < nfx - 1
    side_live = ((lane_id < 64) & in_right) | ((lane_id >= 64) & in_left)
    row_tall = lax.broadcasted_iota(jnp.int32, (tall, 1), 0)
    rows_live = ((row_tall >= 16) | in_top) & ((row_tall < 16 + size) | in_bottom)
    zeros8 = jnp.zeros((8, size), F32)
    for buf in [pa, pb] + [ext.at[c] for c in range(n_chan)]:
        for t in range(2):
            buf[t, 0:8, :] = zeros8
            buf[t, 8 + tall : 16 + tall, :] = zeros8
    spans = [(8, 8 + tall, 32), (8, 8 + tall, 32), (16, tall, 48), (24, 24 + size, 32)]
    pieces = [(0, 0, 16, 1), (16, 16, mid, 0), (16 + mid, 16, mid, 1), (16 + size, 16 + mid, 16, 0)]

    blk_copies = []
    for h in range(halves):
        for copy in halo_copies[h]:
            copy.wait_recv()
        from_left = vl[h].astype(F32)
        from_right = vr[h].astype(F32)
        for q in range(per):
            c = h * per + q
            ext[c, 0, 8:24, :] = jnp.where(in_top, top_recv[h, q].astype(F32), 0.0)
            ext[c, 0, 24 + size : 40 + size, :] = jnp.where(
                in_bottom, bot_recv[h, q].astype(F32), 0.0
            )
            for to, start, count, fold in pieces:
                at = fold * mid + 32 * q
                r = pltpu.roll(from_right[start : start + count], (2 * size - at - 16) % size, 1)
                l = pltpu.roll(from_left[start : start + count], (2 * size - at - 16) % size, 1)
                side = jnp.where(lane_id < 16, r, jnp.where(lane_id >= size - 16, l, 0.0))
                side = jnp.where(rows_live[to : to + count] & side_live, side, 0.0)
                ext[c, 1, 8 + to : 8 + to + count, :] = side
        for q in range(per):
            c = h * per + q
            source = ext.at[c]
            for level in range(len(spans)):
                s = 2**level
                low, top, chunk = spans[level]
                final = level == len(spans) - 1
                dest = None if final else (pa, pb)[level % 2]
                bound = thr_s[level, c]
                for at in range(low, top, chunk):
                    tiles = []
                    for t in range(2):
                        tiles.append(
                            (
                                source[t, at - s : at - s + chunk, :]
                                + 2.0 * source[t, at : at + chunk, :]
                                + source[t, at + s : at + s + chunk, :]
                            )
                            * 0.25
                        )
                    rr = [pltpu.roll(v, s, 1) for v in tiles]
                    ll = [pltpu.roll(v, size - s, 1) for v in tiles]
                    lo_lane, hi_lane = lane_id < s, lane_id >= size - s
                    smooth = (
                        jnp.where(lo_lane, rr[1], rr[0])
                        + 2.0 * tiles[0]
                        + jnp.where(hi_lane, ll[1], ll[0])
                    ) * 0.25
                    if not final:
                        side = (
                            jnp.where(lo_lane, rr[0], rr[1])
                            + 2.0 * tiles[1]
                            + jnp.where(hi_lane, ll[0], ll[1])
                        ) * 0.25
                        inside = rows_live[at - 8 : at - 8 + chunk]
                        if at < 24 or at + chunk > 24 + size:
                            smooth = jnp.where(inside, smooth, 0.0)
                            side = jnp.where(inside & side_live, side, 0.0)
                        else:
                            side = jnp.where(side_live, side, 0.0)
                        dest[0, at : at + chunk, :] = smooth
                        dest[1, at : at + chunk, :] = side
                    first, stop = max(at, 24), min(at + chunk, 24 + size)
                    detail = source[0, first:stop, :] - smooth[first - at : stop - at]
                    own_rows = slice(first - 24, stop - 24)
                    shr[c, own_rows, :] = shr[c, own_rows, :] - jnp.clip(detail, -bound, bound)
                source = dest
            shr_send[c] = shr[c].astype(BF16)
            copy = pltpu.make_async_remote_copy(
                src_ref=shr_send.at[c],
                dst_ref=shr_recv.at[c],
                send_sem=blk_ssem.at[c],
                recv_sem=blk_rsem.at[c],
                device_id=mate,
                device_id_type=MESH,
            )
            copy.start()
            blk_copies.append(copy)

    for c, copy in enumerate(blk_copies):
        copy.wait_recv()
        other[c] = shr_recv[c]

    for copies in [idx_copies] + row_copies + con_copies + halo_copies + [blk_copies]:
        for copy in copies:
            copy.wait_send()


def last_kernel(shr, other, mu_s, out_ref, gpart, gtot, xs):
    n_chan, size, _ = shr.shape
    total = 2 * n_chan
    chunk = 16
    pairs = [(a, b) for a in range(total) for b in range(a, total)]

    def step(i, sums):
        rows = pl.ds(pl.multiple_of(i * chunk, chunk), chunk)
        vals = [shr[c, rows, :] for c in range(n_chan)]
        vals += [other[c, rows, :].astype(F32) for c in range(n_chan)]
        news = []
        for k, (a, b) in enumerate(pairs):
            prod = vals[a] * vals[b]
            news.append(sums[k] + (prod[:8] + prod[8:]))
        return tuple(news)

    sums = lax.fori_loop(
        0, size // chunk, step, tuple(jnp.zeros((8, size), F32) for _ in pairs)
    )
    for (a, b), value in zip(pairs, sums):
        value = jnp.sum(value, axis=0, keepdims=True)
        gpart[a * total + b : a * total + b + 1, :] = value
        if a != b:
            gpart[b * total + a : b * total + a + 1, :] = value
    gtot[...] = jnp.broadcast_to(jnp.sum(gpart[...], axis=1, keepdims=True), gtot.shape)

    mu = mu_s[0] * float(size * size)
    mat = {}
    for a, b in pairs:
        value = jnp.broadcast_to(gtot[a * total + b : a * total + b + 1, :], (total, size))
        mat[a, b] = value + mu if a == b else value
    rhs = [gtot[c * total : (c + 1) * total, :] for c in range(total)]
    inverse = [None] * total
    for k in range(total):
        inverse[k] = 1.0 / mat[k, k]
        for i in range(k + 1, total):
            factor = mat[k, i] * inverse[k]
            for j in range(i, total):
                mat[i, j] = mat[i, j] - factor * mat[k, j]
            rhs[i] = rhs[i] - factor * rhs[k]
    solved = [None] * total
    for k in range(total - 1, -1, -1):
        value = rhs[k]
        for i in range(k + 1, total):
            value = value - mat[k, i] * solved[i]
        solved[k] = value * inverse[k]
        xs[k * total : (k + 1) * total, :] = solved[k]

    coeffs = [
        [jnp.broadcast_to(xs[c * total + d : c * total + d + 1, :], (8, size)) for c in range(total)]
        for d in range(n_chan)
    ]

    def finish(i, carry):
        rows = pl.ds(pl.multiple_of(i * chunk, chunk), chunk)
        vals = [shr[c, rows, :] for c in range(n_chan)]
        vals += [other[c, rows, :].astype(F32) for c in range(n_chan)]
        for d in range(n_chan):
            for h in range(2):
                value = coeffs[d][0] * vals[0][h * 8 : h * 8 + 8]
                for c in range(1, total):
                    value = value + coeffs[d][c] * vals[c][h * 8 : h * 8 + 8]
                out_ref[d, pl.ds(pl.multiple_of(i * chunk + h * 8, 8), 8), :] = value
        return carry

    lax.fori_loop(0, size // chunk, finish, 0)


def body(sizes, sky, vis, weights, tiles, lists, count, threshold, weight):
    nfx, nfy, nblk, fpb, vt, nnz, halves = sizes
    n_chan, size, _ = sky.shape
    per = n_chan // halves
    rows = per * 2 * vt * nnz
    lanes = nfx * 2 * vt * nnz
    hbm = pl.BlockSpec(memory_space=pltpu.HBM)
    smem = pl.BlockSpec(memory_space=pltpu.SMEM)
    vmem = pl.BlockSpec(memory_space=pltpu.VMEM)
    tall = size + 48
    sem = pltpu.SemaphoreType.DMA
    shr, other = pl.pallas_call(
        functools.partial(kernel, sizes),
        out_shape=[
            jax.ShapeDtypeStruct((n_chan, size, size), F32),
            jax.ShapeDtypeStruct((n_chan, size, size), BF16),
        ],
        in_specs=[hbm] * 5 + [smem, hbm, hbm],
        out_specs=[vmem, vmem],
        scratch_shapes=[
            pltpu.SMEM((vt, nnz, fpb), jnp.int32),
            pltpu.SMEM((fpb,), jnp.int32),
            pltpu.SMEM(threshold.shape, F32),
            pltpu.VMEM((n_chan, size, size), BF16),
            pltpu.VMEM((n_chan, 2, vt * size), BF16),
            pltpu.VMEM((fpb // 2, nnz, vt, size, 2 * size), BF16),
            pltpu.VMEM((2, 2 * size, 2 * size), BF16),
            pltpu.VMEM((nfx, 1, lanes), jnp.int32),
            pltpu.VMEM((nfx, 1, lanes), jnp.int32),
            pltpu.VMEM((2 * size, n_chan * size), BF16),
            pltpu.VMEM((halves, nfx, rows, size), BF16),
            pltpu.VMEM((nfx, rows, size), BF16),
            pltpu.VMEM((nfx, rows, size), BF16),
            pltpu.VMEM((halves, fpb + 1, rows, size), BF16),
            pltpu.VMEM((halves, nfx, rows, size), BF16),
            pltpu.VMEM((halves, nfx, rows, size), BF16),
            pltpu.SMEM((nfx,), jnp.int32),
            pltpu.VMEM((halves, per, size, size), BF16),
            pltpu.VMEM((halves, size // 2, size), BF16),
            pltpu.VMEM((halves, per, 16, size), BF16),
            pltpu.VMEM((halves, per, 16, size), BF16),
            pltpu.VMEM((halves, size // 2 + 32, size), BF16),
            pltpu.VMEM((halves, size // 2 + 32, size), BF16),
            pltpu.VMEM((n_chan, 2, tall, size), F32),
            pltpu.VMEM((2, tall, size), F32),
            pltpu.VMEM((2, tall, size), F32),
            pltpu.VMEM((n_chan, size, size), BF16),
            pltpu.VMEM((n_chan, size, size), BF16),
            sem((6 + fpb * nnz,)),
            sem((nfx,)),
            sem((nfx,)),
            sem((halves, nfx)),
            sem((halves, nfx)),
            sem((halves, nfx)),
            sem((halves, nfx)),
            sem((halves, 8)),
            sem((halves, 8)),
            sem((n_chan,)),
            sem((n_chan,)),
        ],
        compiler_params=pltpu.CompilerParams(
            collective_id=0, has_side_effects=True, vmem_limit_bytes=24 * 2**20
        ),
    )(
        pinned(sky),
        pinned(vis[0, 0]),
        pinned(weights[0, 0]),
        pinned(tiles[0, 0].transpose(1, 2, 0)),
        pinned(lists.reshape(-1)),
        count.reshape(-1),
        pinned(threshold),
        pinned(jnp.asarray(tables(size))),
    )
    square = pltpu.VMEM((4 * n_chan * n_chan, size), F32)
    return pl.pallas_call(
        last_kernel,
        out_shape=jax.ShapeDtypeStruct((n_chan, size, size), F32),
        in_specs=[vmem, vmem, smem],
        out_specs=vmem,
        scratch_shapes=[square, square, square],
        compiler_params=pltpu.CompilerParams(vmem_limit_bytes=8 * 2**20),
    )(shr, other, weight.reshape(1))


def solution(mesh):
    in_specs = (
        P("blk", "fy", "fx"),
        P("fy", "fx", "blk", None, None),
        P("fy", "fx", None, None, None, None, None),
        P("fy", "fx", None, None, None),
        P("fy", "fx", None),
        P("fy", "fx"),
        P(None, "blk"),
        P(),
    )

    def step(*args):
        fpb, vt, nnz = args[3].shape[2:]
        sizes = (mesh.shape["fx"], mesh.shape["fy"], mesh.shape["blk"], fpb, vt, nnz, 2)
        return body(sizes, *args)

    return jax.shard_map(
        step, mesh=mesh, in_specs=in_specs, out_specs=P("blk", "fy", "fx"), check_vma=False
    )
```

time: 58.4 us -> 51.4 us (0.88); the launches traced: 57.4 us -> 51.2 us
  Pallas kernels: 53 us -> 49.9 us
  local copies, waits for them, and re-layouts: 3.08 us -> 0 us
    pallas_call x1 -> x2, Pallas kernels: 53 us -> 49.9 us  [the longest x1 48.5 us: body(): pl.pallas_call(functools.partial(kernel, sizes), out_shape=[jax.ShapeDtyp...]
    unnamed x2 -> x0, local copies, waits for them, and re-layouts: 2.46 us -> none
    reshape x1 -> x0, local copies, waits for them, and re-layouts: 0.62 us -> none  [body(): tiles.reshape(-1)]
where the time goes in v2:
time: 51.4 us; the launch traced here: 51.2 us
  Pallas kernels  49.9 us (97%)
  between operations  1.31 us (3%)
    pallas_call x1, Pallas kernels, body(): pl.pallas_call(functools.partial(kernel, sizes), out_shape=[jax.ShapeDtyp...  48.5 us
    pallas_call x1, Pallas kernels, body(): pl.pallas_call(last_kernel, out_shape=jax.ShapeDtypeStruct((n_chan, size,...  1.38 us

profile of v2, /device:TPU:1, one launch (start us, length us, event | category | flops | bytes accessed | tf_op | source)
XLA Modules:
  0.0 51.2 jit_solution(11402067113291542030)
XLA Ops:
  1.3 48.5 %shard_map.91 = (f32[4,128,128]{2,1,0:T(8,128)S(1)}, bf16[4,128,128]{2,1,0:T(8,128)(2,1)S(1)}) custom-call(bf16[4,128,128]{2,1,0:T(8,128)(2,1)} %sky_hbm.1, bf16[4,2,512]{2,1,0:T(2,128)(2,1)} %bitcast.11, bf16[8,4,2,128,128]{4,3,2,1,0:T(8,128)(2,1)} %bitcast.10, s32[4,2,8]{2,1,0:T(2,128)} %bitcast.12, s32[8]{0:T(128)} %bitcast.13, s32[1]{0:T(128)} %bitcast.8.count_s, ...), custom_call_target="tpu_custom_call" | custom-call | tf_op jit(solution)/shard_map/pallas_call | solution.py:541
  49.8 1.4 %shard_map.92 = f32[4,128,128]{2,1,0:T(8,128)} custom-call(f32[4,128,128]{2,1,0:T(8,128)S(1)} %get-tuple-element.7.shr, bf16[4,128,128]{2,1,0:T(8,128)(2,1)S(1)} %get-tuple-element.8.other, f32[1]{0:T(128)} %bitcast.9.mu_s), custom_call_target="tpu_custom_call" | custom-call | tf_op jit(solution)/shard_map/pallas_call | solution.py:604

commit v3 on v2

v3 whole, which is shorter than its diff:
```python
import functools
import math

import jax
import jax.numpy as jnp
import ml_dtypes
import numpy as np
from jax import lax
from jax.experimental import pallas as pl
from jax.experimental.pallas import tpu as pltpu
from jax.sharding import PartitionSpec as P

MESH = pl.DeviceIdType.MESH
F32 = jnp.float32
BF16 = jnp.bfloat16
STEP = 2.0


def tables(length):
    positions = np.arange(length)
    angles = (positions[:, None] * positions[None, :] % length) * (2.0 * math.pi / length)
    cosine = (np.cos(angles) / math.sqrt(length)).astype(np.float32)
    sinus = (np.sin(angles) / math.sqrt(length)).astype(np.float32)
    whole = np.concatenate(
        [np.concatenate([cosine, -sinus], axis=1), np.concatenate([sinus, cosine], axis=1)], axis=0
    )
    high = whole.astype(ml_dtypes.bfloat16)
    low = (whole - high.astype(np.float32)).astype(ml_dtypes.bfloat16)
    return np.stack([high, low])


def smoothers(size, levels, margin):
    reach = np.arange(-2 * margin, size + 2 * margin)
    apart = np.abs(reach[:, None] - reach[None, :])
    out = np.zeros((3, 2 * size, levels * size), np.float64)
    for variant in range(3):
        alive = np.ones(len(reach))
        if variant == 0:
            alive[reach < 0] = 0
        if variant == 2:
            alive[reach >= size] = 0
        whole = np.diag(alive)
        for level in range(levels):
            one = 2.0 * (apart == 0) + 1.0 * (apart == 2**level)
            whole = alive[:, None] * (one @ whole)
            taps = (whole / 16.0 ** (level + 1))[2 * margin : 2 * margin + size].T
            span = slice(level * size, (level + 1) * size)
            out[variant, :size, span] = taps[2 * margin : 2 * margin + size]
            out[variant, size : size + margin, span] = taps[2 * margin + size : 3 * margin + size]
            out[variant, 2 * size - margin :, span] = taps[margin : 2 * margin]
    return out.astype(ml_dtypes.bfloat16)


def dot(a, b):
    return jnp.dot(a, b, preferred_element_type=F32)


def dot_nt(a, b):
    return lax.dot_general(a, b, (((1,), (1,)), ((), ())), preferred_element_type=F32)


def dot_tn(a, b):
    return lax.dot_general(a, b, (((0,), (0,)), ((), ())), preferred_element_type=F32)


def split(values):
    high = values.astype(BF16)
    return high, (values - high.astype(F32)).astype(BF16)


def dot3(a, b):
    return dot(a[0], b[0]) + (dot(a[0], b[1]) + dot(a[1], b[0]))


def pinned(array):
    return pltpu.with_memory_space_constraint(array, pltpu.HBM)


def kernel(
    sizes,
    sky_hbm,
    vis_hbm,
    w_hbm,
    tiles_hbm,
    list_hbm,
    count_s,
    thr_hbm,
    tab_hbm,
    smooth_hbm,
    shr,
    other,
    tiles_s,
    list_s,
    sky_v,
    vis_v,
    wv,
    tab,
    smooth,
    idx_send,
    idx_recv,
    spec,
    row_send,
    row_recv0,
    row_recv1,
    con_buf,
    con_send,
    con_recv,
    inv_s,
    slot_s,
    place_mat,
    st_bf,
    mate_bf,
    edge_send,
    top_recv,
    bot_recv,
    vl,
    vr,
    hi_buf,
    ybuf,
    zbuf,
    thr_v,
    thr_mate,
    bounds,
    local_sem,
    idx_ssem,
    idx_rsem,
    row_ssem,
    row_rsem,
    con_ssem,
    con_rsem,
    halo_ssem,
    halo_rsem,
    thr_sem,
):
    nfx, nfy, nblk, fpb, vt, nnz, halves = sizes
    n_chan, size, _ = sky_v.shape
    per = n_chan // halves
    row_recv = (row_recv0, row_recv1)
    slots = vt * nnz
    lanes = nfx * 2 * slots
    fy, fx, blk = lax.axis_index("fy"), lax.axis_index("fx"), lax.axis_index("blk")

    def along_fx(d):
        return (fy, lax.rem(fx + d, nfx), blk)

    up, down = lax.rem(fy + nfy - 1, nfy), lax.rem(fy + 1, nfy)
    left, right = lax.rem(fx + nfx - 1, nfx), lax.rem(fx + 1, nfx)
    mate = (fy, fx, 1 - blk)
    order = sorted(range(1, nfx), key=lambda d: -min(d, nfx - d))
    far = [d for d in order if min(d, nfx - d) > nfx // 4]
    near = [d for d in order if d not in far]
    slot = {d: k for k, d in enumerate([0] + near + far)}

    loads = []

    def load(src, dst):
        copy = pltpu.make_async_copy(src, dst, local_sem.at[len(loads)])
        copy.start()
        loads.append(copy)
        return copy

    barrier = pltpu.get_barrier_semaphore()
    others = [along_fx(d) for d in order]
    around = [(up, fx), (down, fx), (fy, left), (fy, right)]
    around += [(r, c) for r in (up, down) for c in (left, right)]
    others += [(up, fx, blk), (down, fx, blk), mate]
    others += [(r, c, blk) for r in (up, down) for c in (left, right)]
    others += [(r, c, 1 - blk) for r, c in around]
    for device in others:
        pl.semaphore_signal(barrier, inc=1, device_id=device, device_id_type=MESH)

    small_loads = [
        load(tiles_hbm, tiles_s),
        load(list_hbm, list_s),
    ]
    thr_load = load(thr_hbm, thr_v)
    tab_load = load(tab_hbm, tab)
    sky_load = load(sky_hbm, sky_v)
    vis_load = load(vis_hbm, vis_v)
    w_loads = [
        load(w_hbm.at[f, :, n], wv.at[f // 2, n, :, :, pl.ds((f % 2) * size, size)])
        for f in range(fpb)
        for n in range(nnz)
    ]
    edge_kind = (fx + nfx - 2) // (nfx - 1) + fx // (nfx - 1)
    smooth_load = load(smooth_hbm.at[edge_kind], smooth)

    for copy in small_loads:
        copy.wait()
    lane = lax.broadcasted_iota(jnp.int32, (1, lanes), 1)
    lane_a, lane_n = lane % vt, (lane // vt) % nnz
    lane_p, lane_j = (lane // slots) % 2, lane // (2 * slots)
    wanted = []
    for f in range(fpb):
        row = jnp.zeros((1, lanes), jnp.int32)
        for a in range(vt):
            for n in range(nnz):
                here = (lane_a == a) & (lane_n == n)
                row = jnp.where(here, tiles_s[a, n, f], row)
        wanted.append(row + lane_p * size + 1)
    where_f = [0] * fpb
    for d in range(nfx):
        owner = lax.rem(fx + d, nfx)
        request = jnp.zeros((1, lanes), jnp.int32)
        place = fpb
        for f in range(fpb):
            hit = list_s[f] == owner
            request = jnp.where(hit, wanted[f], request)
            place = jnp.where(hit, f, place)
            where_f[f] = jnp.where(hit, slot[d], where_f[f])
        idx_send[slot[d]] = jnp.where(lane_j == slot[d], request, 0)
        inv_s[slot[d]] = place
    for f in range(fpb):
        slot_s[f] = where_f[f]
    idx_recv[0] = idx_send[0]

    pl.semaphore_wait(barrier, len(others))

    def exchange(send, recv, ssem, rsem, sign=1, peers=order):
        copies = []
        for d in peers:
            copy = pltpu.make_async_remote_copy(
                src_ref=send.at[slot[d]],
                dst_ref=recv.at[slot[d]],
                send_sem=ssem.at[d],
                recv_sem=rsem.at[d],
                device_id=along_fx(d if sign > 0 else nfx - d),
                device_id_type=MESH,
            )
            copy.start()
            copies.append(copy)
        return copies

    idx_copies = exchange(idx_send, idx_recv, idx_ssem, idx_rsem)
    thr_load.wait()
    thr_copy = pltpu.make_async_remote_copy(
        src_ref=thr_v,
        dst_ref=thr_mate,
        send_sem=thr_sem.at[0],
        recv_sem=thr_sem.at[1],
        device_id=mate,
        device_id_type=MESH,
    )
    thr_copy.start()

    tab_load.wait()
    sky_load.wait()
    high = tab[0]
    left_table = jnp.concatenate([high[:size, :size], high[:size, size:]], axis=0)
    for c in range(n_chan):
        half = dot(left_table, sky_v[c]).astype(BF16)
        half = jnp.concatenate([half[:size], half[size:]], axis=1)
        full = dot(half, high).astype(BF16)
        spec[:size, c * size : (c + 1) * size] = full[:, :size]
        spec[size:, c * size : (c + 1) * size] = full[:, size:]

    row_ids = lax.broadcasted_iota(jnp.int32, (2 * size, lanes), 0) + 1
    group = 2 * slots
    row_copies = [[] for _ in range(halves)]
    for k, peers in enumerate((near, far)):
        for copy, d in zip(idx_copies, order):
            if d in peers:
                copy.wait_recv()
        first, count = (0, 1 + len(near)) if k == 0 else (1 + len(near), len(far))
        span_k = slice(first * group, (first + count) * group)
        target = idx_recv[first, :, span_k]
        for e in range(first + 1, first + count):
            target = target + idx_recv[e, :, span_k]
        mat = jnp.where(row_ids[:, : count * group] == target, 1.0, 0.0).astype(BF16)
        place_mat[:, span_k] = mat
        for h in range(halves):
            span = slice(h * per * size, (h + 1) * per * size)
            picked = dot_tn(mat, spec[:, span]).reshape(count, 2, 1, slots, per * size)
            picked = jnp.concatenate(
                [picked[..., c * size : (c + 1) * size] for c in range(per)], axis=2
            )
            row_send[h, first : first + count] = picked.reshape(count, per * group, size).astype(BF16)
            if k == 0:
                row_recv[h][0] = row_send[h, 0]
            row_copies[h] += exchange(
                row_send.at[h], row_recv[h], row_ssem.at[h], row_rsem.at[h], -1, peers
            )

    rows_all = per * group
    n_vis = vt * size
    vis_load.wait()
    row_id = lax.broadcasted_iota(jnp.int32, (rows_all, n_vis), 0)
    vis_id = lax.broadcasted_iota(jnp.int32, (rows_all, n_vis), 1)
    live = (vis_id < count_s[0]) & (row_id % vt == vis_id // size)
    first_slot = (row_id // vt) % nnz == 0
    first_out = (lax.broadcasted_iota(jnp.int32, (rows_all, 2 * size), 0) // vt) % nnz == 0
    for h in range(halves):
        con_buf[h, fpb] = jnp.zeros((rows_all, size), BF16)
    for copy in w_loads:
        copy.wait()

    con_copies = []
    for h in range(halves):
        for copy in row_copies[h]:
            copy.wait_recv()
        measured = []
        for p in range(2):
            for c in range(per):
                both = vis_v[h * per + c].astype(F32)
                measured.append(jnp.broadcast_to(both[p : p + 1], (slots, n_vis)))
        measured = jnp.concatenate(measured, axis=0)
        sums = [None, None]
        for q in range(fpb // 2):
            x = jnp.concatenate(
                [row_recv[h][slot_s[2 * q]], row_recv[h][slot_s[2 * q + 1]]], axis=1
            )
            for n in range(nnz):
                term = dot_nt(x, wv[q, n].reshape(n_vis, 2 * size))
                sums[n] = term if sums[n] is None else sums[n] + term
        mixed = jnp.where(first_slot, sums[0], sums[1])
        later = pltpu.roll(mixed, rows_all - vt, 0)
        earlier = pltpu.roll(mixed, vt, 0)
        predicted = mixed + jnp.where(first_slot, later, earlier)
        residual = jnp.where(live, predicted - measured, 0.0).astype(BF16)
        for q in range(fpb // 2):
            terms = [dot(residual, wv[q, n].reshape(n_vis, 2 * size)) for n in range(nnz)]
            out = jnp.where(first_out, terms[0], terms[1]).astype(BF16)
            con_buf[h, 2 * q] = out[:, :size]
            con_buf[h, 2 * q + 1] = out[:, size:]
        for k in range(nfx):
            con_send[h, k] = con_buf[h, inv_s[k]]
        con_recv[h, 0] = con_send[h, 0]
        con_copies.append(
            exchange(con_send.at[h], con_recv.at[h], con_ssem.at[h], con_rsem.at[h])
        )

    def flipped(table):
        return jnp.concatenate(
            [
                jnp.concatenate([table[:size, :size], table[size:, :size]], axis=1),
                jnp.concatenate([table[:size, size:], table[size:, size:]], axis=1),
            ],
            axis=0,
        )

    right_back = (flipped(tab[0]), flipped(tab[1]))
    left_back = tuple(dot(tab[k, :size, :], place_mat[...]).astype(BF16) for k in range(2))
    lane_id = lax.broadcasted_iota(jnp.int32, (1, size), 1)
    quarter = size // 4
    halo_copies = []
    for h in range(halves):
        for copy in con_copies[h]:
            copy.wait_recv()
        own_rows = per * slots
        incoming = jnp.concatenate(
            [
                con_recv[h, :, p * own_rows : (p + 1) * own_rows, :].reshape(nfx * own_rows, size)
                for p in range(2)
            ],
            axis=1,
        )
        half = dot(incoming, right_back[0]) + dot(incoming, right_back[1])
        half = half.reshape(nfx, per, slots, 2 * size)
        half = jnp.concatenate(
            [
                jnp.concatenate(
                    [half[:, c : c + 1, :, p * size : (p + 1) * size] for p in range(2)], axis=1
                ).reshape(nfx * group, size)
                for c in range(per)
            ],
            axis=1,
        )
        grad = dot3(left_back, split(half))
        edges = [jnp.zeros((quarter, size), F32) for _ in range(2)]
        for c in range(per):
            stepped = sky_v[h * per + c].astype(F32) - STEP * grad[:, c * size : (c + 1) * size]
            shr[h * per + c] = stepped
            high = stepped.astype(BF16)
            st_bf[h, c] = high
            hi_buf[h, c, 16 : 16 + size, :size] = high
            for fold in range(4):
                at = 32 * fold + 16 * c
                part = stepped[fold * quarter : (fold + 1) * quarter]
                hit = (lane_id >= at) & (lane_id < at + 16)
                for e, turn in enumerate((at, (at + 16) % size)):
                    moved = pltpu.roll(part, turn, 1) if turn else part
                    edges[e] = jnp.where(hit, moved, edges[e])
        for e in range(2):
            edge_send[h, e] = edges[e].astype(BF16)

        first, last = pl.ds(0, 16), pl.ds(quarter - 16, 16)
        main, low = pl.ds(16, quarter), pl.ds(16 + quarter, 16)
        copies = []

        def send(src, dst, device, who, k):
            copy = pltpu.make_async_remote_copy(
                src_ref=src,
                dst_ref=dst,
                send_sem=halo_ssem.at[h, who, k],
                recv_sem=halo_rsem.at[h, who, k],
                device_id=device,
                device_id_type=MESH,
            )
            copy.start()
            copies.append(copy)

        send(st_bf.at[h], mate_bf.at[h], mate, 1, 8)
        for who, where in ((0, blk), (1, 1 - blk)):
            top, bottom = top_recv.at[h, who], bot_recv.at[h, who]
            fl, fr = vl.at[h, who], vr.at[h, who]
            halo = [
                (edge_send.at[h, 0, first], fr.at[low], (up, left, where)),
                (edge_send.at[h, 1, first], fl.at[low], (up, right, where)),
                (edge_send.at[h, 0, last], fr.at[first], (down, left, where)),
                (edge_send.at[h, 1, last], fl.at[first], (down, right, where)),
                (edge_send.at[h, 0], fr.at[main], (fy, left, where)),
                (edge_send.at[h, 1], fl.at[main], (fy, right, where)),
                (st_bf.at[h, :, pl.ds(0, 16), :], bottom, (up, fx, where)),
                (st_bf.at[h, :, pl.ds(size - 16, 16), :], top, (down, fx, where)),
            ]
            for k, (src, dst, device) in enumerate(halo):
                send(src, dst, device, who, k)
        halo_copies.append(copies)

    tall = size + 32
    streams = 2 * per
    in_top, in_bottom = fy > 0, fy < nfy - 1
    row_tall = lax.broadcasted_iota(jnp.int32, (tall, 1), 0)
    rows_live = ((row_tall >= 16) | in_top) & ((row_tall < 16 + size) | in_bottom)
    zeros8 = jnp.zeros((8, size), F32)
    levels = thr_v.shape[0]
    thr_copy.wait_recv()
    for who, part in enumerate((thr_v, thr_mate)):
        for c in range(n_chan):
            for level in range(levels):
                at = (who * n_chan + c) * levels + level
                value = part[level : level + 1, c : c + 1]
                bounds[at : at + 1, :] = jnp.broadcast_to(value, (1, size))
    for buf in (ybuf, zbuf):
        for q in range(streams):
            for level in range(1, levels):
                buf[q, level, 0:8, :] = zeros8
                buf[q, level, 8 + tall : 16 + tall, :] = zeros8
    smooth_load.wait()
    for copies in [idx_copies, [thr_copy]] + row_copies + con_copies:
        for copy in copies:
            copy.wait_send()
    pieces = [(0, 0, 16, 3), (16 + size, 16 + quarter, 16, 0)]
    pieces += [(16 + k * quarter, 16, quarter, k) for k in range(4)]

    def summed(ref, at, count, s):
        x = ref[at : at + count, :]
        return (ref[at - s : at - s + count, :] + x) + (ref[at + s : at + s + count, :] + x)

    for h in range(halves):
        for copy in halo_copies[h]:
            copy.wait_recv()
        for who in range(2):
            from_left = vl[h, who].astype(F32)
            from_right = vr[h, who].astype(F32)
            for c in range(per):
                q = who * per + c
                if who == 1:
                    hi_buf[h, q, 16 : 16 + size, :size] = mate_bf[h, c]
                hi_buf[h, q, 0:16, :size] = jnp.where(
                    in_top, top_recv[h, who, c].astype(F32), 0.0
                ).astype(BF16)
                hi_buf[h, q, 16 + size :, :size] = jnp.where(
                    in_bottom, bot_recv[h, who, c].astype(F32), 0.0
                ).astype(BF16)
                for to, start, count, fold in pieces:
                    at = 32 * fold + 16 * c
                    r = from_right[start : start + count]
                    r = pltpu.roll(r, size - at, 1) if at else r
                    l = pltpu.roll(from_left[start : start + count], (2 * size - 16 - at) % size, 1)
                    side = jnp.where(lane_id < 64, r, l)
                    if to in (0, 16 + size):
                        side = jnp.where(rows_live[to : to + count], side, 0.0)
                    hi_buf[h, q, to : to + count, size:] = side.astype(BF16)
        for t in range(levels // 2):
            span = slice(2 * t * size, 2 * (t + 1) * size)
            result = dot(hi_buf[h].reshape(streams * tall, 2 * size), smooth[:, span])
            for q in range(streams):
                for e in range(2):
                    ybuf[q, 2 * t + e, 8 : 8 + tall, :] = result[
                        q * tall : (q + 1) * tall, e * size : (e + 1) * size
                    ]
        for q in range(streams):
            who, c = q // per, h * per + q % per
            sources = [ybuf.at[q, 0]]
            for level in range(1, levels):
                source, dest = ybuf.at[q, level], zbuf.at[q, level]
                reach = 2 ** (level + 1) - 2
                for step in range(level):
                    s = 2**step
                    reach -= s if step else 0
                    low, top = (24 - reach) // 8 * 8, (24 + size + reach + 7) // 8 * 8
                    for at, stop in ((low, 24), (24 + size, top)):
                        part = summed(source, at, stop - at, s)
                        dest[at:stop, :] = jnp.where(rows_live[at - 8 : stop - 8], part, 0.0)
                    for at in range(24, 24 + size, 32):
                        dest[at : at + 32, :] = summed(source, at, 32, s)
                    source, dest = dest, source
                sources.append(source)
            for at in range(0, size, 16):
                rows = slice(at, at + 16)
                value = shr[c, rows, :] if who == 0 else mate_bf[h, q % per, rows, :].astype(F32)
                coarse = value
                for level in range(levels):
                    at_bound = (who * n_chan + c) * levels + level
                    bound = bounds[at_bound : at_bound + 1, :]
                    finer = summed(sources[level], 24 + at, 16, 2**level)
                    value = value - jnp.minimum(jnp.maximum(coarse - finer, -bound), bound)
                    coarse = finer
                if who == 0:
                    shr[c, rows, :] = value
                else:
                    other[c, rows, :] = value

    for copies in halo_copies:
        for copy in copies:
            copy.wait_send()


def last_kernel(shr, other, mu_s, out_ref, gpart, gtot, xs):
    n_chan, size, _ = shr.shape
    total = 2 * n_chan
    chunk = 16
    pairs = [(a, b) for a in range(total) for b in range(a, total)]

    def step(i, sums):
        rows = pl.ds(pl.multiple_of(i * chunk, chunk), chunk)
        vals = [shr[c, rows, :] for c in range(n_chan)]
        vals += [other[c, rows, :].astype(F32) for c in range(n_chan)]
        news = []
        for k, (a, b) in enumerate(pairs):
            prod = vals[a] * vals[b]
            news.append(sums[k] + (prod[:8] + prod[8:]))
        return tuple(news)

    sums = lax.fori_loop(
        0, size // chunk, step, tuple(jnp.zeros((8, size), F32) for _ in pairs)
    )
    for (a, b), value in zip(pairs, sums):
        value = jnp.sum(value, axis=0, keepdims=True)
        gpart[a * total + b : a * total + b + 1, :] = value
        if a != b:
            gpart[b * total + a : b * total + a + 1, :] = value
    gtot[...] = jnp.broadcast_to(jnp.sum(gpart[...], axis=1, keepdims=True), gtot.shape)

    mu = mu_s[0] * float(size * size)
    mat = {}
    for a, b in pairs:
        value = jnp.broadcast_to(gtot[a * total + b : a * total + b + 1, :], (total, size))
        mat[a, b] = value + mu if a == b else value
    rhs = [gtot[c * total : (c + 1) * total, :] for c in range(total)]
    inverse = [None] * total
    for k in range(total):
        inverse[k] = 1.0 / mat[k, k]
        for i in range(k + 1, total):
            factor = mat[k, i] * inverse[k]
            for j in range(i, total):
                mat[i, j] = mat[i, j] - factor * mat[k, j]
            rhs[i] = rhs[i] - factor * rhs[k]
    solved = [None] * total
    for k in range(total - 1, -1, -1):
        value = rhs[k]
        for i in range(k + 1, total):
            value = value - mat[k, i] * solved[i]
        solved[k] = value * inverse[k]
        xs[k * total : (k + 1) * total, :] = solved[k]

    coeffs = [
        [jnp.broadcast_to(xs[c * total + d : c * total + d + 1, :], (8, size)) for c in range(total)]
        for d in range(n_chan)
    ]

    def finish(i, carry):
        rows = pl.ds(pl.multiple_of(i * chunk, chunk), chunk)
        vals = [shr[c, rows, :] for c in range(n_chan)]
        vals += [other[c, rows, :].astype(F32) for c in range(n_chan)]
        for d in range(n_chan):
            for h in range(2):
                value = coeffs[d][0] * vals[0][h * 8 : h * 8 + 8]
                for c in range(1, total):
                    value = value + coeffs[d][c] * vals[c][h * 8 : h * 8 + 8]
                out_ref[d, pl.ds(pl.multiple_of(i * chunk + h * 8, 8), 8), :] = value
        return carry

    lax.fori_loop(0, size // chunk, finish, 0)


def body(sizes, sky, vis, weights, tiles, lists, count, threshold, weight):
    nfx, nfy, nblk, fpb, vt, nnz, halves = sizes
    n_chan, size, _ = sky.shape
    per = n_chan // halves
    rows = per * 2 * vt * nnz
    lanes = nfx * 2 * vt * nnz
    hbm = pl.BlockSpec(memory_space=pltpu.HBM)
    smem = pl.BlockSpec(memory_space=pltpu.SMEM)
    vmem = pl.BlockSpec(memory_space=pltpu.VMEM)
    tall = size + 48
    levels = threshold.shape[0]
    sem = pltpu.SemaphoreType.DMA
    shr, other = pl.pallas_call(
        functools.partial(kernel, sizes),
        out_shape=[
            jax.ShapeDtypeStruct((n_chan, size, size), F32),
            jax.ShapeDtypeStruct((n_chan, size, size), F32),
        ],
        in_specs=[hbm] * 5 + [smem, hbm, hbm, hbm],
        out_specs=[vmem, vmem],
        scratch_shapes=[
            pltpu.SMEM((vt, nnz, fpb), jnp.int32),
            pltpu.SMEM((fpb,), jnp.int32),
            pltpu.VMEM((n_chan, size, size), BF16),
            pltpu.VMEM((n_chan, 2, vt * size), BF16),
            pltpu.VMEM((fpb // 2, nnz, vt, size, 2 * size), BF16),
            pltpu.VMEM((2, 2 * size, 2 * size), BF16),
            pltpu.VMEM((2 * size, levels * size), BF16),
            pltpu.VMEM((nfx, 1, lanes), jnp.int32),
            pltpu.VMEM((nfx, 1, lanes), jnp.int32),
            pltpu.VMEM((2 * size, n_chan * size), BF16),
            pltpu.VMEM((halves, nfx, rows, size), BF16),
            pltpu.VMEM((nfx, rows, size), BF16),
            pltpu.VMEM((nfx, rows, size), BF16),
            pltpu.VMEM((halves, fpb + 1, rows, size), BF16),
            pltpu.VMEM((halves, nfx, rows, size), BF16),
            pltpu.VMEM((halves, nfx, rows, size), BF16),
            pltpu.SMEM((nfx,), jnp.int32),
            pltpu.SMEM((fpb,), jnp.int32),
            pltpu.VMEM((2 * size, lanes), BF16),
            pltpu.VMEM((halves, per, size, size), BF16),
            pltpu.VMEM((halves, per, size, size), BF16),
            pltpu.VMEM((halves, 2, size // 4, size), BF16),
            pltpu.VMEM((halves, 2, per, 16, size), BF16),
            pltpu.VMEM((halves, 2, per, 16, size), BF16),
            pltpu.VMEM((halves, 2, size // 4 + 32, size), BF16),
            pltpu.VMEM((halves, 2, size // 4 + 32, size), BF16),
            pltpu.VMEM((halves, 2 * per, size + 32, 2 * size), BF16),
            pltpu.VMEM((2 * per, levels, tall, size), F32),
            pltpu.VMEM((2 * per, levels, tall, size), F32),
            pltpu.VMEM(threshold.shape, F32),
            pltpu.VMEM(threshold.shape, F32),
            pltpu.VMEM((2 * n_chan * levels, size), F32),
            sem((7 + fpb * nnz,)),
            sem((nfx,)),
            sem((nfx,)),
            sem((halves, nfx)),
            sem((halves, nfx)),
            sem((halves, nfx)),
            sem((halves, nfx)),
            sem((halves, 2, 9)),
            sem((halves, 2, 9)),
            sem((2,)),
        ],
        compiler_params=pltpu.CompilerParams(
            collective_id=0, has_side_effects=True, vmem_limit_bytes=24 * 2**20
        ),
    )(
        pinned(sky),
        pinned(vis[0, 0]),
        pinned(weights[0, 0]),
        pinned(tiles[0, 0].transpose(1, 2, 0)),
        pinned(lists.reshape(-1)),
        count.reshape(-1),
        pinned(threshold),
        pinned(jnp.asarray(tables(size))),
        pinned(jnp.asarray(smoothers(size, levels, 16))),
    )
    square = pltpu.VMEM((4 * n_chan * n_chan, size), F32)
    return pl.pallas_call(
        last_kernel,
        out_shape=jax.ShapeDtypeStruct((n_chan, size, size), F32),
        in_specs=[vmem, vmem, smem],
        out_specs=vmem,
        scratch_shapes=[square, square, square],
        compiler_params=pltpu.CompilerParams(vmem_limit_bytes=8 * 2**20),
    )(shr, other, weight.reshape(1))


def solution(mesh):
    in_specs = (
        P("blk", "fy", "fx"),
        P("fy", "fx", "blk", None, None),
        P("fy", "fx", None, None, None, None, None),
        P("fy", "fx", None, None, None),
        P("fy", "fx", None),
        P("fy", "fx"),
        P(None, "blk"),
        P(),
    )

    def step(*args):
        fpb, vt, nnz = args[3].shape[2:]
        sizes = (mesh.shape["fx"], mesh.shape["fy"], mesh.shape["blk"], fpb, vt, nnz, 2)
        return body(sizes, *args)

    return jax.shard_map(
        step, mesh=mesh, in_specs=in_specs, out_specs=P("blk", "fy", "fx"), check_vma=False
    )
```

time: 51.4 us -> 50.2 us (0.977)
  Pallas kernels: 49.9 us -> 48.8 us
    pallas_call x1, Pallas kernels: 48.5 us -> 47.4 us  [body(): pl.pallas_call(functools.partial(kernel, sizes), out_shape=[jax.ShapeDtyp...]
where the time goes in v3:
time: 50.2 us; the launch traced here: 50.1 us
  Pallas kernels  48.8 us (97%)
  between operations  1.31 us (3%)
    pallas_call x1, Pallas kernels, body(): pl.pallas_call(functools.partial(kernel, sizes), out_shape=[jax.ShapeDtyp...  47.4 us
    pallas_call x1, Pallas kernels, body(): pl.pallas_call(last_kernel, out_shape=jax.ShapeDtypeStruct((n_chan, size,...  1.39 us

profile of v3, /device:TPU:1, one launch (start us, length us, event | category | flops | bytes accessed | tf_op | source)
XLA Modules:
  0.0 50.1 jit_solution(7715031362090385977)
XLA Ops:
  1.3 47.4 %shard_map.100 = (f32[4,128,128]{2,1,0:T(8,128)S(1)}, f32[4,128,128]{2,1,0:T(8,128)S(1)}) custom-call(bf16[4,128,128]{2,1,0:T(8,128)(2,1)} %sky_hbm.1, bf16[4,2,512]{2,1,0:T(2,128)(2,1)} %bitcast.11, bf16[8,4,2,128,128]{4,3,2,1,0:T(8,128)(2,1)} %bitcast.10, s32[4,2,8]{2,1,0:T(2,128)} %bitcast.12, s32[8]{0:T(128)} %bitcast.13, s32[1]{0:T(128)} %bitcast.8.count_s, ...), custom_call_target="tpu_custom_call" | custom-call | tf_op jit(solution)/shard_map/pallas_call | solution.py:600
  48.7 1.4 %shard_map.101 = f32[4,128,128]{2,1,0:T(8,128)} custom-call(f32[4,128,128]{2,1,0:T(8,128)S(1)} %get-tuple-element.7.shr, f32[4,128,128]{2,1,0:T(8,128)S(1)} %get-tuple-element.8.other, f32[1]{0:T(128)} %bitcast.9.mu_s), custom_call_target="tpu_custom_call" | custom-call | tf_op jit(solution)/shard_map/pallas_call | solution.py:667

commit v4 on v3

--- a/solution.py
+++ b/solution.py
@@ -109,12 +109,8 @@
     slot_s,
     place_mat,
     st_bf,
-    mate_bf,
     edge_send,
-    top_recv,
-    bot_recv,
-    vl,
-    vr,
+    halo_recv,
     hi_buf,
     ybuf,
     zbuf,
@@ -153,6 +149,9 @@
 
     loads = []
 
+    def arrived(buffer, semaphore):
+        pltpu.make_async_copy(buffer, buffer, semaphore).wait()
+
     def load(src, dst):
         copy = pltpu.make_async_copy(src, dst, local_sem.at[len(loads)])
         copy.start()
@@ -177,11 +176,13 @@
     tab_load = load(tab_hbm, tab)
     sky_load = load(sky_hbm, sky_v)
     vis_load = load(vis_hbm, vis_v)
-    w_loads = [
-        load(w_hbm.at[f, :, n], wv.at[f // 2, n, :, :, pl.ds((f % 2) * size, size)])
-        for f in range(fpb)
-        for n in range(nnz)
-    ]
+    for f in range(fpb):
+        for n in range(nnz):
+            pltpu.make_async_copy(
+                w_hbm.at[f, :, n],
+                wv.at[f // 2, n, :, :, pl.ds((f % 2) * size, size)],
+                local_sem.at[local_sem.shape[0] - 1],
+            ).start()
     edge_kind = (fx + nfx - 2) // (nfx - 1) + fx // (nfx - 1)
     smooth_load = load(smooth_hbm.at[edge_kind], smooth)
 
@@ -217,21 +218,18 @@
     pl.semaphore_wait(barrier, len(others))
 
     def exchange(send, recv, ssem, rsem, sign=1, peers=order):
-        copies = []
         for d in peers:
-            copy = pltpu.make_async_remote_copy(
+            pltpu.make_async_remote_copy(
                 src_ref=send.at[slot[d]],
                 dst_ref=recv.at[slot[d]],
-                send_sem=ssem.at[d],
-                recv_sem=rsem.at[d],
+                send_sem=ssem,
+                recv_sem=rsem if peers is order or sign < 0 else rsem.at[int(d in far)],
                 device_id=along_fx(d if sign > 0 else nfx - d),
                 device_id_type=MESH,
-            )
-            copy.start()
-            copies.append(copy)
-        return copies
-
-    idx_copies = exchange(idx_send, idx_recv, idx_ssem, idx_rsem)
+            ).start()
+
+    exchange(idx_send, idx_recv, idx_ssem.at[0], idx_rsem, 1, far)
+    exchange(idx_send, idx_recv, idx_ssem.at[0], idx_rsem, 1, near)
     thr_load.wait()
     thr_copy = pltpu.make_async_remote_copy(
         src_ref=thr_v,
@@ -256,48 +254,48 @@
 
     row_ids = lax.broadcasted_iota(jnp.int32, (2 * size, lanes), 0) + 1
     group = 2 * slots
-    row_copies = [[] for _ in range(halves)]
-    for k, peers in enumerate((near, far)):
-        for copy, d in zip(idx_copies, order):
-            if d in peers:
-                copy.wait_recv()
-        first, count = (0, 1 + len(near)) if k == 0 else (1 + len(near), len(far))
+    groups = ((0, 1 + len(near), near), (1 + len(near), len(far), far))
+
+    def answer(k, h):
+        first, count, peers = groups[k]
+        mat = place_mat[:, first * group : (first + count) * group]
+        span = slice(h * per * size, (h + 1) * per * size)
+        picked = dot_tn(mat, spec[:, span]).reshape(count, 2, 1, slots, per * size)
+        picked = jnp.concatenate(
+            [picked[..., c * size : (c + 1) * size] for c in range(per)], axis=2
+        )
+        row_send[h, first : first + count] = picked.reshape(count, per * group, size).astype(BF16)
+        if k == 0:
+            row_recv[h][0] = row_send[h, 0]
+        exchange(row_send.at[h], row_recv[h], row_ssem.at[h], row_rsem.at[h], -1, peers)
+
+    for k, (first, count, peers) in enumerate(groups):
+        arrived(idx_recv.at[pl.ds(first + (k == 0), len(peers))], idx_rsem.at[k])
         span_k = slice(first * group, (first + count) * group)
         target = idx_recv[first, :, span_k]
         for e in range(first + 1, first + count):
             target = target + idx_recv[e, :, span_k]
         mat = jnp.where(row_ids[:, : count * group] == target, 1.0, 0.0).astype(BF16)
         place_mat[:, span_k] = mat
-        for h in range(halves):
-            span = slice(h * per * size, (h + 1) * per * size)
-            picked = dot_tn(mat, spec[:, span]).reshape(count, 2, 1, slots, per * size)
-            picked = jnp.concatenate(
-                [picked[..., c * size : (c + 1) * size] for c in range(per)], axis=2
-            )
-            row_send[h, first : first + count] = picked.reshape(count, per * group, size).astype(BF16)
-            if k == 0:
-                row_recv[h][0] = row_send[h, 0]
-            row_copies[h] += exchange(
-                row_send.at[h], row_recv[h], row_ssem.at[h], row_rsem.at[h], -1, peers
-            )
+        answer(k, 0)
+    for h in range(1, halves):
+        for k in (1, 0):
+            answer(k, h)
 
     rows_all = per * group
     n_vis = vt * size
     vis_load.wait()
     row_id = lax.broadcasted_iota(jnp.int32, (rows_all, n_vis), 0)
     vis_id = lax.broadcasted_iota(jnp.int32, (rows_all, n_vis), 1)
-    live = (vis_id < count_s[0]) & (row_id % vt == vis_id // size)
+    live = (vis_id < count_s[0, 0]) & (row_id % vt == vis_id // size)
     first_slot = (row_id // vt) % nnz == 0
     first_out = (lax.broadcasted_iota(jnp.int32, (rows_all, 2 * size), 0) // vt) % nnz == 0
     for h in range(halves):
         con_buf[h, fpb] = jnp.zeros((rows_all, size), BF16)
-    for copy in w_loads:
-        copy.wait()
-
-    con_copies = []
+    arrived(wv, local_sem.at[local_sem.shape[0] - 1])
+
     for h in range(halves):
-        for copy in row_copies[h]:
-            copy.wait_recv()
+        arrived(row_recv[h].at[pl.ds(1, nfx - 1)], row_rsem.at[h])
         measured = []
         for p in range(2):
             for c in range(per):
@@ -325,9 +323,7 @@
         for k in range(nfx):
             con_send[h, k] = con_buf[h, inv_s[k]]
         con_recv[h, 0] = con_send[h, 0]
-        con_copies.append(
-            exchange(con_send.at[h], con_recv.at[h], con_ssem.at[h], con_rsem.at[h])
-        )
+        exchange(con_send.at[h], con_recv.at[h], con_ssem.at[h], con_rsem.at[h])
 
     def flipped(table):
         return jnp.concatenate(
@@ -342,10 +338,9 @@
     left_back = tuple(dot(tab[k, :size, :], place_mat[...]).astype(BF16) for k in range(2))
     lane_id = lax.broadcasted_iota(jnp.int32, (1, size), 1)
     quarter = size // 4
-    halo_copies = []
+    block = 2 * (quarter + 32) + 2 * per * 16
     for h in range(halves):
-        for copy in con_copies[h]:
-            copy.wait_recv()
+        arrived(con_recv.at[h, pl.ds(1, nfx - 1)], con_rsem.at[h])
         own_rows = per * slots
         incoming = jnp.concatenate(
             [
@@ -384,38 +379,31 @@
             edge_send[h, e] = edges[e].astype(BF16)
 
         first, last = pl.ds(0, 16), pl.ds(quarter - 16, 16)
-        main, low = pl.ds(16, quarter), pl.ds(16 + quarter, 16)
-        copies = []
-
-        def send(src, dst, device, who, k):
-            copy = pltpu.make_async_remote_copy(
+        def send(src, at, count, device):
+            pltpu.make_async_remote_copy(
                 src_ref=src,
-                dst_ref=dst,
-                send_sem=halo_ssem.at[h, who, k],
-                recv_sem=halo_rsem.at[h, who, k],
+                dst_ref=halo_recv.at[h, pl.ds(at, count)],
+                send_sem=halo_ssem.at[h],
+                recv_sem=halo_rsem.at[h],
                 device_id=device,
                 device_id_type=MESH,
-            )
-            copy.start()
-            copies.append(copy)
-
-        send(st_bf.at[h], mate_bf.at[h], mate, 1, 8)
+            ).start()
+
+        for c in range(per):
+            send(st_bf.at[h, c], c * size, size, mate)
         for who, where in ((0, blk), (1, 1 - blk)):
-            top, bottom = top_recv.at[h, who], bot_recv.at[h, who]
-            fl, fr = vl.at[h, who], vr.at[h, who]
-            halo = [
-                (edge_send.at[h, 0, first], fr.at[low], (up, left, where)),
-                (edge_send.at[h, 1, first], fl.at[low], (up, right, where)),
-                (edge_send.at[h, 0, last], fr.at[first], (down, left, where)),
-                (edge_send.at[h, 1, last], fl.at[first], (down, right, where)),
-                (edge_send.at[h, 0], fr.at[main], (fy, left, where)),
-                (edge_send.at[h, 1], fl.at[main], (fy, right, where)),
-                (st_bf.at[h, :, pl.ds(0, 16), :], bottom, (up, fx, where)),
-                (st_bf.at[h, :, pl.ds(size - 16, 16), :], top, (down, fx, where)),
-            ]
-            for k, (src, dst, device) in enumerate(halo):
-                send(src, dst, device, who, k)
-        halo_copies.append(copies)
+            fr = per * size + who * block
+            fl, top = fr + quarter + 32, fr + 2 * (quarter + 32)
+            bottom = top + per * 16
+            send(edge_send.at[h, 0, first], fr + 16 + quarter, 16, (up, left, where))
+            send(edge_send.at[h, 1, first], fl + 16 + quarter, 16, (up, right, where))
+            send(edge_send.at[h, 0, last], fr, 16, (down, left, where))
+            send(edge_send.at[h, 1, last], fl, 16, (down, right, where))
+            send(edge_send.at[h, 0], fr + 16, quarter, (fy, left, where))
+            send(edge_send.at[h, 1], fl + 16, quarter, (fy, right, where))
+            for c in range(per):
+                send(st_bf.at[h, c, pl.ds(0, 16)], bottom + 16 * c, 16, (up, fx, where))
+                send(st_bf.at[h, c, pl.ds(size - 16, 16)], top + 16 * c, 16, (down, fx, where))
 
     tall = size + 32
     streams = 2 * per
@@ -437,9 +425,11 @@
                 buf[q, level, 0:8, :] = zeros8
                 buf[q, level, 8 + tall : 16 + tall, :] = zeros8
     smooth_load.wait()
-    for copies in [idx_copies, [thr_copy]] + row_copies + con_copies:
-        for copy in copies:
-            copy.wait_send()
+    thr_copy.wait_send()
+    arrived(idx_send.at[pl.ds(1, nfx - 1)], idx_ssem.at[0])
+    for h in range(halves):
+        arrived(row_send.at[h, pl.ds(1, nfx - 1)], row_ssem.at[h])
+        arrived(con_send.at[h, pl.ds(1, nfx - 1)], con_ssem.at[h])
     pieces = [(0, 0, 16, 3), (16 + size, 16 + quarter, 16, 0)]
     pieces += [(16 + k * quarter, 16, quarter, k) for k in range(4)]
 
@@ -448,20 +438,22 @@
         return (ref[at - s : at - s + count, :] + x) + (ref[at + s : at + s + count, :] + x)
 
     for h in range(halves):
-        for copy in halo_copies[h]:
-            copy.wait_recv()
+        arrived(halo_recv.at[h], halo_rsem.at[h])
         for who in range(2):
-            from_left = vl[h, who].astype(F32)
-            from_right = vr[h, who].astype(F32)
+            fr = per * size + who * block
+            fl, top = fr + quarter + 32, fr + 2 * (quarter + 32)
+            bottom = top + per * 16
+            from_left = halo_recv[h, fl : fl + quarter + 32].astype(F32)
+            from_right = halo_recv[h, fr : fr + quarter + 32].astype(F32)
             for c in range(per):
                 q = who * per + c
                 if who == 1:
-                    hi_buf[h, q, 16 : 16 + size, :size] = mate_bf[h, c]
+                    hi_buf[h, q, 16 : 16 + size, :size] = halo_recv[h, c * size : (c + 1) * size]
                 hi_buf[h, q, 0:16, :size] = jnp.where(
-                    in_top, top_recv[h, who, c].astype(F32), 0.0
+                    in_top, halo_recv[h, top + 16 * c : top + 16 * c + 16].astype(F32), 0.0
                 ).astype(BF16)
                 hi_buf[h, q, 16 + size :, :size] = jnp.where(
-                    in_bottom, bot_recv[h, who, c].astype(F32), 0.0
+                    in_bottom, halo_recv[h, bottom + 16 * c : bottom + 16 * c + 16].astype(F32), 0.0
                 ).astype(BF16)
                 for to, start, count, fold in pieces:
                     at = 32 * fold + 16 * c
@@ -499,7 +491,8 @@
                 sources.append(source)
             for at in range(0, size, 16):
                 rows = slice(at, at + 16)
-                value = shr[c, rows, :] if who == 0 else mate_bf[h, q % per, rows, :].astype(F32)
+                base = (q % per) * size + at
+                value = shr[c, rows, :] if who == 0 else halo_recv[h, base : base + 16].astype(F32)
                 coarse = value
                 for level in range(levels):
                     at_bound = (who * n_chan + c) * levels + level
@@ -512,9 +505,8 @@
                 else:
                     other[c, rows, :] = value
 
-    for copies in halo_copies:
-        for copy in copies:
-            copy.wait_send()
+    for h in range(halves):
+        arrived(halo_recv.at[h], halo_ssem.at[h])
 
 
 def last_kernel(shr, other, mu_s, out_ref, gpart, gtot, xs):
@@ -626,27 +618,23 @@
             pltpu.SMEM((fpb,), jnp.int32),
             pltpu.VMEM((2 * size, lanes), BF16),
             pltpu.VMEM((halves, per, size, size), BF16),
-            pltpu.VMEM((halves, per, size, size), BF16),
             pltpu.VMEM((halves, 2, size // 4, size), BF16),
-            pltpu.VMEM((halves, 2, per, 16, size), BF16),
-            pltpu.VMEM((halves, 2, per, 16, size), BF16),
-            pltpu.VMEM((halves, 2, size // 4 + 32, size), BF16),
-            pltpu.VMEM((halves, 2, size // 4 + 32, size), BF16),
+            pltpu.VMEM((halves, per * size + 4 * (size // 4 + 32 + per * 16), size), BF16),
             pltpu.VMEM((halves, 2 * per, size + 32, 2 * size), BF16),
             pltpu.VMEM((2 * per, levels, tall, size), F32),
             pltpu.VMEM((2 * per, levels, tall, size), F32),
             pltpu.VMEM(threshold.shape, F32),
             pltpu.VMEM(threshold.shape, F32),
             pltpu.VMEM((2 * n_chan * levels, size), F32),
-            sem((7 + fpb * nnz,)),
-            sem((nfx,)),
-            sem((nfx,)),
-            sem((halves, nfx)),
-            sem((halves, nfx)),
-            sem((halves, nfx)),
-            sem((halves, nfx)),
-            sem((halves, 2, 9)),
-            sem((halves, 2, 9)),
+            sem((9,)),
+            sem((1,)),
+            sem((2,)),
+            sem((halves,)),
+            sem((halves,)),
+            sem((halves,)),
+            sem((halves,)),
+            sem((halves,)),
+            sem((halves,)),
             sem((2,)),
         ],
         compiler_params=pltpu.CompilerParams(
@@ -658,7 +646,7 @@
         pinned(weights[0, 0]),
         pinned(tiles[0, 0].transpose(1, 2, 0)),
         pinned(lists.reshape(-1)),
-        count.reshape(-1),
+        count,
         pinned(threshold),
         pinned(jnp.asarray(tables(size))),
         pinned(jnp.asarray(smoothers(size, levels, 16))),

time: 50.2 us -> 47.2 us (0.940)
  Pallas kernels: 48.8 us -> 45.8 us
    pallas_call x1, Pallas kernels: 47.4 us -> 44.4 us  [body(): pl.pallas_call(functools.partial(kernel, sizes), out_shape=[jax.ShapeDtyp...]
where the time goes in v4:
time: 47.2 us; the launch traced here: 47.1 us
  Pallas kernels  45.8 us (97%)
  between operations  1.31 us (3%)
    pallas_call x1, Pallas kernels, body(): pl.pallas_call(functools.partial(kernel, sizes), out_shape=[jax.ShapeDtyp...  44.4 us
    pallas_call x1, Pallas kernels, body(): pl.pallas_call(last_kernel, out_shape=jax.ShapeDtypeStruct((n_chan, size,...  1.39 us

profile of v4, /device:TPU:1, one launch (start us, length us, event | category | flops | bytes accessed | tf_op | source)
XLA Modules:
  0.0 47.1 jit_solution(10833277506249746546)
XLA Ops:
  1.3 44.4 %shard_map.100 = (f32[4,128,128]{2,1,0:T(8,128)S(1)}, f32[4,128,128]{2,1,0:T(8,128)S(1)}) custom-call(bf16[4,128,128]{2,1,0:T(8,128)(2,1)} %sky_hbm.1, bf16[4,2,512]{2,1,0:T(2,128)(2,1)} %bitcast.9, bf16[8,4,2,128,128]{4,3,2,1,0:T(8,128)(2,1)} %bitcast.8, s32[4,2,8]{2,1,0:T(2,128)} %bitcast.10, s32[8]{0:T(128)} %bitcast.11, s32[1,1]{1,0:T(1,128)S(6)} %copy.14.count_s, ...), custom_call_target="tpu_custom_call" | custom-call | tf_op jit(solution)/shard_map/pallas_call | solution.py:592
  45.7 1.4 %shard_map.101 = f32[4,128,128]{2,1,0:T(8,128)} custom-call(f32[4,128,128]{2,1,0:T(8,128)S(1)} %get-tuple-element.7.shr, f32[4,128,128]{2,1,0:T(8,128)S(1)} %get-tuple-element.8.other, f32[1]{0:T(128)} %bitcast.7.mu_s), custom_call_target="tpu_custom_call" | custom-call | tf_op jit(solution)/shard_map/pallas_call | solution.py:655

commit v5 on v4

--- a/solution.py
+++ b/solution.py
@@ -389,8 +389,6 @@
                 device_id_type=MESH,
             ).start()
 
-        for c in range(per):
-            send(st_bf.at[h, c], c * size, size, mate)
         for who, where in ((0, blk), (1, 1 - blk)):
             fr = per * size + who * block
             fl, top = fr + quarter + 32, fr + 2 * (quarter + 32)
@@ -404,6 +402,8 @@
             for c in range(per):
                 send(st_bf.at[h, c, pl.ds(0, 16)], bottom + 16 * c, 16, (up, fx, where))
                 send(st_bf.at[h, c, pl.ds(size - 16, 16)], top + 16 * c, 16, (down, fx, where))
+        for c in range(per):
+            send(st_bf.at[h, c], c * size, size, mate)
 
     tall = size + 32
     streams = 2 * per
@@ -509,7 +509,7 @@
         arrived(halo_recv.at[h], halo_ssem.at[h])
 
 
-def last_kernel(shr, other, mu_s, out_ref, gpart, gtot, xs):
+def last_kernel(shr, other, mu_s, out_hbm, out_ref, gpart, gtot, xs, out_sem):
     n_chan, size, _ = shr.shape
     total = 2 * n_chan
     chunk = 16
@@ -574,7 +574,19 @@
                 out_ref[d, pl.ds(pl.multiple_of(i * chunk + h * 8, 8), 8), :] = value
         return carry
 
-    lax.fori_loop(0, size // chunk, finish, 0)
+    parts = 4
+    each = size // chunk // parts
+    copies = []
+    for part in range(parts):
+        lax.fori_loop(part * each, (part + 1) * each, finish, 0)
+        rows = pl.ds(part * each * chunk, each * chunk)
+        copy = pltpu.make_async_copy(
+            out_ref.at[:, rows, :], out_hbm.at[:, rows, :], out_sem.at[part]
+        )
+        copy.start()
+        copies.append(copy)
+    for copy in copies:
+        copy.wait()
 
 
 def body(sizes, sky, vis, weights, tiles, lists, count, threshold, weight):
@@ -656,8 +668,8 @@
         last_kernel,
         out_shape=jax.ShapeDtypeStruct((n_chan, size, size), F32),
         in_specs=[vmem, vmem, smem],
-        out_specs=vmem,
-        scratch_shapes=[square, square, square],
+        out_specs=hbm,
+        scratch_shapes=[pltpu.VMEM((n_chan, size, size), F32), square, square, square, sem((4,))],
         compiler_params=pltpu.CompilerParams(vmem_limit_bytes=8 * 2**20),
     )(shr, other, weight.reshape(1))
 

time: 47.2 us -> 47.2 us (level)
  no operation moved by 1% of the time
where the time goes in v5:
time: 47.2 us; the launch traced here: 47.1 us
  Pallas kernels  45.8 us (97%)
  between operations  1.31 us (3%)
    pallas_call x1, Pallas kernels, body(): pl.pallas_call(functools.partial(kernel, sizes), out_shape=[jax.ShapeDtyp...  44.4 us
    pallas_call x1, Pallas kernels, body(): pl.pallas_call(last_kernel, out_shape=jax.ShapeDtypeStruct((n_chan, size,...  1.33 us

profile of v5, /device:TPU:1, one launch (start us, length us, event | category | flops | bytes accessed | tf_op | source)
XLA Modules:
  0.0 47.1 jit_solution(5320086184153383630)
XLA Ops:
  1.3 44.4 %shard_map.100 = (f32[4,128,128]{2,1,0:T(8,128)S(1)}, f32[4,128,128]{2,1,0:T(8,128)S(1)}) custom-call(bf16[4,128,128]{2,1,0:T(8,128)(2,1)} %sky_hbm.1, bf16[4,2,512]{2,1,0:T(2,128)(2,1)} %bitcast.9, bf16[8,4,2,128,128]{4,3,2,1,0:T(8,128)(2,1)} %bitcast.8, s32[4,2,8]{2,1,0:T(2,128)} %bitcast.10, s32[8]{0:T(128)} %bitcast.11, s32[1,1]{1,0:T(1,128)S(6)} %copy.14.count_s, ...), custom_call_target="tpu_custom_call" | custom-call | tf_op jit(solution)/shard_map/pallas_call | solution.py:604
  45.7 1.3 %shard_map.101 = f32[4,128,128]{2,1,0:T(8,128)} custom-call(f32[4,128,128]{2,1,0:T(8,128)S(1)} %get-tuple-element.7.shr, f32[4,128,128]{2,1,0:T(8,128)S(1)} %get-tuple-element.8.other, f32[1]{0:T(128)} %bitcast.7.mu_s), custom_call_target="tpu_custom_call" | custom-call | tf_op jit(solution)/shard_map/pallas_call | solution.py:667

commit v6 on v4

--- a/solution.py
+++ b/solution.py
@@ -143,7 +143,7 @@
     left, right = lax.rem(fx + nfx - 1, nfx), lax.rem(fx + 1, nfx)
     mate = (fy, fx, 1 - blk)
     order = sorted(range(1, nfx), key=lambda d: -min(d, nfx - d))
-    far = [d for d in order if min(d, nfx - d) > nfx // 4]
+    far = [d for d in order if min(d, nfx - d) > 3 * nfx // 8]
     near = [d for d in order if d not in far]
     slot = {d: k for k, d in enumerate([0] + near + far)}
 

time: 47.2 us -> 48.1 us (1.019)
  Pallas kernels: 45.8 us -> 46.5 us
    pallas_call x1, Pallas kernels: 44.4 us -> 45.2 us  [body(): pl.pallas_call(functools.partial(kernel, sizes), out_shape=[jax.ShapeDtyp...]
where the time goes in v6:
time: 48.1 us; the launch traced here: 47.9 us
  Pallas kernels  46.5 us (97%)
  between operations  1.31 us (3%)
    pallas_call x1, Pallas kernels, body(): pl.pallas_call(functools.partial(kernel, sizes), out_shape=[jax.ShapeDtyp...  45.2 us
    pallas_call x1, Pallas kernels, body(): pl.pallas_call(last_kernel, out_shape=jax.ShapeDtypeStruct((n_chan, size,...  1.39 us

profile of v6, /device:TPU:1, one launch (start us, length us, event | category | flops | bytes accessed | tf_op | source)
XLA Modules:
  0.0 47.9 jit_solution(2672664570023705223)
XLA Ops:
  1.3 45.2 %shard_map.100 = (f32[4,128,128]{2,1,0:T(8,128)S(1)}, f32[4,128,128]{2,1,0:T(8,128)S(1)}) custom-call(bf16[4,128,128]{2,1,0:T(8,128)(2,1)} %sky_hbm.1, bf16[4,2,512]{2,1,0:T(2,128)(2,1)} %bitcast.9, bf16[8,4,2,128,128]{4,3,2,1,0:T(8,128)(2,1)} %bitcast.8, s32[4,2,8]{2,1,0:T(2,128)} %bitcast.10, s32[8]{0:T(128)} %bitcast.11, s32[1,1]{1,0:T(1,128)S(6)} %copy.14.count_s, ...), custom_call_target="tpu_custom_call" | custom-call | tf_op jit(solution)/shard_map/pallas_call | solution.py:592
  46.5 1.4 %shard_map.101 = f32[4,128,128]{2,1,0:T(8,128)} custom-call(f32[4,128,128]{2,1,0:T(8,128)S(1)} %get-tuple-element.7.shr, f32[4,128,128]{2,1,0:T(8,128)S(1)} %get-tuple-element.8.other, f32[1]{0:T(128)} %bitcast.7.mu_s), custom_call_target="tpu_custom_call" | custom-call | tf_op jit(solution)/shard_map/pallas_call | solution.py:655
